TPU v7x, 256 devices: a whole 4x4x8 slice. The times are simulated.
256 devices in a mesh: gx: 16 (over y_hi, z), gy: 16 (over y_lo, x, core).
Axes of the slice: x: 4, y: 4 (y_hi: 2, y_lo: 2; y = y_hi * 2 + y_lo), z: 8, core: 2. Of those that a mesh axis runs over, the one named last changes fastest.
Arguments:
- hidden: bfloat16 [8192, 14336], P('gx', 'gy'), may hold values from -6 to 6
- weight: bfloat16 [4096, 14336], P(None, 'gy'), may hold values from -0.0625 to 0.0625
- cotangent: bfloat16 [8192, 4096], P('gx', 'gy'), may hold values from -6 to 6
Outputs:
- output: bfloat16 [8192, 4096], P('gx', 'gy')
- hidden_grad: bfloat16 [8192, 14336], P('gx', 'gy')
- weight_grad: float32 [4096, 14336], P('gx', 'gy')
All inputs are finite; a program needn't handle non-finite values.
Results may differ from a plain program's by a relative error of at most 0.001.
Values may be sent and summed in bfloat16 or wider, within the bound.
No kernel may reach another device: no remote copies, remote signals or barrier semaphores. Data moves between devices by JAX's collectives and lax.ppermute only.
A program may use at most 128 MiB of HBM per device.

v0:
```python
import jax
import jax.numpy as jnp
from jax import lax
from jax.sharding import Mesh
from jax.sharding import PartitionSpec as P

GX = ("gx_0", "gx_1")
GY = ("gy_0", "gy_1", "gy_2")


def in_blocks(array, dim, devices):
    dims = array.shape
    blocks = array.reshape(*dims[:dim], devices, dims[dim] // devices, *dims[dim + 1 :])
    return jnp.moveaxis(blocks, dim, 0)


def summed_on_arrival(array, axis, dim):
    blocks = in_blocks(array, dim, lax.axis_size(axis))
    arrived = lax.all_to_all(blocks, axis, split_axis=0, concat_axis=0, tiled=True)
    return arrived.sum(axis=0)


def summed_rows(array, axes, dim):
    far, near = axes
    blocks = in_blocks(array, dim, lax.axis_size(far))
    nearer = summed_on_arrival(blocks, near, dim + 1)
    arrived = lax.all_to_all(nearer, far, split_axis=0, concat_axis=0, tiled=True)
    return arrived.sum(axis=0)


def from_everyone(array, axis):
    copies = jnp.broadcast_to(array, (lax.axis_size(axis), *array.shape))
    return lax.all_to_all(copies, axis, split_axis=0, concat_axis=0, tiled=True)


def joined_along(blocks, dim):
    dims = list(blocks.shape[1:])
    dims[dim] *= blocks.shape[0]
    return jnp.moveaxis(blocks, 0, dim).reshape(dims)


def whole_of(array, axes, dim):
    far, near = axes
    leading = from_everyone(array, far)
    blocks = jnp.swapaxes(from_everyone(leading, near), 0, 1)
    return joined_along(blocks.reshape(-1, *array.shape), dim)


def sum_in_order(blocks, axes, order):
    dims = [lax.axis_size(a) for a in axes]
    blocks = blocks.reshape(*dims, *blocks.shape[1:])
    blocks = blocks.transpose(*order, *range(len(axes), blocks.ndim))
    blocks = blocks.reshape(-1, *blocks.shape[len(axes) :])
    for k in order:
        blocks = lax.psum_scatter(blocks, axes[k], scatter_dimension=0, tiled=True)
    return blocks[0]


def scatter_axes(array, axes, order, dim):
    devices = lax.axis_size(axes)
    return sum_in_order(in_blocks(array, dim, devices), axes, order)


def shards(hidden, weight, cotangent):
    tok_rows = hidden.shape[0]
    grad_scale = float(tok_rows * lax.axis_size(GX)) ** (-0.5)
    output_rows = summed_rows(
        lax.dot_general(
            weight, hidden, (((1,), (1,)), ((), ())), preferred_element_type=jnp.float32
        ),
        (("gy_0", "gy_1"), "gy_2"),
        0,
    )
    output = output_rows.T.astype(jnp.bfloat16)
    cotangent_full = whole_of(cotangent, (("gy_0", "gy_1"), "gy_2"), 1)
    hidden_grad = jnp.dot(cotangent_full, weight, preferred_element_type=jnp.float32).astype(
        jnp.bfloat16
    )
    summed = scatter_axes(
        lax.dot_general(
            cotangent_full, hidden, (((0,), (0,)), ((), ())), preferred_element_type=jnp.float32
        ),
        GX,
        (1, 0),
        0,
    )
    weight_grad = summed * grad_scale
    return (output, hidden_grad, weight_grad)


def solution(mesh):
    finer = Mesh(mesh.devices.reshape(2, 8, 2, 4, 2), ("gx_0", "gx_1", "gy_0", "gy_1", "gy_2"))
    placed = (P(GX, GY), P(None, GY), P(GX, GY))
    return jax.shard_map(
        shards,
        mesh=finer,
        in_specs=placed,
        out_specs=(P(GX, GY), P(GX, GY), P(GX, GY)),
        check_vma=False,
    )
```

profile of v0, /device:TPU:1, one launch (start us, length us, event | category | flops | bytes accessed | tf_op | source)
XLA Modules:
  0.0 285.7 jit_solution(610249531185500054)
XLA Ops:
  7.2 0.0 copy-start
  7.2 0.0 reduce-scatter.3.cloned.1.call-start
  7.2 1.2 copy.22
  8.4 0.2 broadcast_in_dim.6
  8.6 31.8 %all_to_all.20 = bf16[8,512,256]{1,2,0:T(8,128)(2,1)S(1)} all-to-all(bf16[8,512,256]{1,2,0:T(8,128)(2,1)S(1)} %broadcast_in_dim.6), channel_id=1, replica_groups=mesh['gx_0'=2,'gx_1'=8,'gy_0'=2,'gy_1'=4,'gy_2'=2] {'gy_0','gy_1'}, dimensions={0} | all-to-all | bytes 4194304 | tf_op jit(solution)/shard_map/all_to_all | solution.py:33
  40.4 0.5 broadcast_in_dim.7
  40.8 9.5 %all_to_all.21 = bf16[2,8,512,256]{2,3,1,0:T(8,128)(2,1)} all-to-all(bf16[2,8,512,256]{2,3,1,0:T(8,128)(2,1)S(1)} %broadcast_in_dim.7), channel_id=1, replica_groups=mesh['gx_0'=2,'gx_1'=8,'gy_0'=2,'gy_1'=4,'gy_2'=2] {'gy_2'}, dimensions={0} | all-to-all | bytes 8388608 | tf_op jit(solution)/shard_map/all_to_all | solution.py:33
  50.4 6.4 %copy.23 = bf16[2,8,512,256]{3,2,0,1:T(8,128)(2,1)} copy(bf16[2,8,512,256]{2,3,1,0:T(8,128)(2,1)} %all_to_all.21) | data formatting | bytes 8388608 | tf_op jit(solution)/shard_map/all_to_all | solution.py:33
  56.8 6.4 %copy.24 = bf16[512,16,256]{0,2,1:T(8,128)(2,1)} copy(bf16[512,16,256]{2,0,1:T(8,128)(2,1)} %bitcast.34) | data formatting | bytes 8388608 | tf_op jit(solution)/shard_map/transpose | solution.py:39
  63.2 0.0 copy-done
  63.2 9.8 %convolution_bitcast_fusion = f32[8,2,256,896]{3,2,0,1:T(8,128)} fusion(bf16[2,8,256,512]{3,2,1,0:T(8,128)(2,1)} %bitcast.36, bf16[512,896]{1,0:T(8,128)(2,1)S(1)} %copy-done), kind=kOutput, calls=%fused_computation.1 | convolution fusion | flops 3758096384 | bytes 19791872 | tf_op jit(solution)/shard_map/dot_general | solution.py:80
  73.0 11.8 %copy.25 = f32[8,2,256,896]{3,2,1,0:T(8,128)} copy(f32[8,2,256,896]{3,2,0,1:T(8,128)} %convolution_bitcast_fusion) | data formatting | bytes 29360128 | tf_op jit(solution)/shard_map/transpose | solution.py:52
  84.8 0.0 reduce-scatter.3.cloned.1.call-update
  84.9 6.9 %fusion.1 = f32[4096,512]{1,0:T(8,128)S(1)} fusion(bf16[4096,896]{1,0:T(8,128)(2,1)} %param.4, bf16[512,896]{1,0:T(8,128)(2,1)S(1)} %copy-done), kind=kOutput, calls=%fused_computation.6 | convolution fusion | flops 3758096384 | bytes 16646144 | tf_op jit(solution)/shard_map/dot_general | solution.py:68
  91.8 1.3 copy.29
  93.2 11.8 %all_to_all.22 = f32[2,8,256,512]{3,2,1,0:T(8,128)} all-to-all(f32[2,8,256,512]{3,2,1,0:T(8,128)S(1)} %bitcast.33), channel_id=1, replica_groups=mesh['gx_0'=2,'gx_1'=8,'gy_0'=2,'gy_1'=4,'gy_2'=2] {'gy_2'}, dimensions={0} | all-to-all | bytes 16777216 | tf_op jit(solution)/shard_map/all_to_all | solution.py:19
  105.0 7.0 %reduce_sum.18 = f32[8,256,512]{2,1,0:T(8,128)} reduce(f32[2,8,256,512]{3,2,1,0:T(8,128)} %all_to_all.22, f32[]{:T(128)} %constant.0.clone.1), dimensions={0}, to_apply=%region_0.0 | reduce | flops 1048576 | bytes 12582916 | tf_op jit(solution)/shard_map/reduce_sum | solution.py:20
  112.0 4.6 %all-to-all-start.1 = ((f32[8,256,512]{2,1,0:T(8,128)}), f32[8,256,512]{2,1,0:T(8,128)}, u32[]{:S(2)}, u32[]{:S(2)}) async-start(f32[8,256,512]{2,1,0:T(8,128)} %reduce_sum.18), calls=%async_computation.1 | async-start | bytes 8388608 | tf_op jit(solution)/shard_map/all_to_all | solution.py:27
  116.6 0.2 reduce-scatter.5.cloned.1.call-start
  116.8 123.2 %reduce-scatter.3.cloned.1.call-done = f32[2,256,896]{2,1,0:T(8,128)} async-done(((f32[16,256,896]{2,1,0:T(8,128)}), f32[2,256,896]{2,1,0:T(8,128)}) %reduce-scatter.3.cloned.1.call-update) | async-done | bytes 1835024 | tf_op jit(solution)/shard_map/reduce_scatter | solution.py:55
  240.0 0.0 reduce-scatter.5.cloned.1.call-update
  240.0 0.0 copy-start.1
  240.0 9.9 %convolution_convert_fusion = bf16[512,896]{1,0:T(8,128)(2,1)} fusion(bf16[512,4096]{0,1:T(8,128)(2,1)} %bitcast.37, bf16[4096,896]{1,0:T(8,128)(2,1)} %param.4), kind=kOutput, calls=%fused_computation.2 | convolution fusion | flops 3758555136 | bytes 12451840 | tf_op jit(solution)/shard_map/dot_general | solution.py:76
  249.9 0.0 all-to-all-done.1
  249.9 2.7 reduce_sum.19
  252.6 0.8 copy.26
  253.4 23.3 %reduce-scatter.5.cloned.1.call-done = f32[1,256,896]{2,1,0:T(8,128)} async-done(((f32[2,256,896]{2,1,0:T(8,128)}), f32[1,256,896]{2,1,0:T(8,128)}) %reduce-scatter.5.cloned.1.call-update) | async-done | bytes 917520 | tf_op jit(solution)/shard_map/reduce_scatter | solution.py:55
  276.7 2.2 multiply_bitcast_fusion
  278.9 0.0 copy-done.1
Async XLA Ops:
  7.2 56.1 %copy-start = (bf16[512,896]{1,0:T(8,128)(2,1)S(1)}, bf16[512,896]{1,0:T(8,128)(2,1)}, u32[]{:S(2)}) copy-start(bf16[512,896]{1,0:T(8,128)(2,1)} %param.3) | copy-start | bytes 2752516
  7.2 232.8 %reduce-scatter.3.cloned.1.call-start = ((), (), s32[]{:S(2)}) async-start(), calls=%async_computation.6 | async-start | bytes 16515072 | tf_op jit(solution)/shard_map/reduce_scatter | solution.py:55
  112.0 137.9 %all-to-all-start.1 = ((f32[8,256,512]{2,1,0:T(8,128)}), f32[8,256,512]{2,1,0:T(8,128)}, u32[]{:S(2)}, u32[]{:S(2)}) async-start(f32[8,256,512]{2,1,0:T(8,128)} %reduce_sum.18), calls=%async_computation.1 | async-start | bytes 8388608 | tf_op jit(solution)/shard_map/all_to_all | solution.py:27
  116.6 160.1 %reduce-scatter.5.cloned.1.call-start = ((), (), s32[]{:S(2)}) async-start(), calls=%async_computation.7 | async-start | bytes 2752512 | tf_op jit(solution)/shard_map/reduce_scatter | solution.py:55
  240.0 38.9 %copy-start.1 = (bf16[512,896]{1,0:T(8,128)(2,1)S(1)}, bf16[512,896]{1,0:T(8,128)(2,1)}, u32[]{:S(2)}) copy-start(bf16[512,896]{1,0:T(8,128)(2,1)} %param.3) | copy-start | bytes 2752516
Sparse Core Ops, SparseCore 0:
  85.0 154.9 reduce-scatter.2
  242.5 34.1 reduce-scatter.4
where the time goes:
time: 286 us
  waiting for transfers between devices  146 us (51%)
  blocking collectives  53.1 us (19%)
  local copies, waits for them, and re-layouts  28.7 us (10%)
  matrix products  26.6 us (9%)
  between operations  14.1 us (5%)
  other arithmetic  11.9 us (4%)
  starting transfers between devices  4.83 us (2%)
    reduce_scatter x2, waiting for transfers between devices, sum_in_order(): blocks = lax.psum_scatter(blocks, axes[k], scatter_dimension=0, tiled=True)  146 us
    all_to_all x2, blocking collectives, from_everyone(): return lax.all_to_all(copies, axis, split_axis=0, concat_axis=0, tiled=True)  41.3 us
    transpose x1, local copies, waits for them, and re-layouts, sum_in_order(): blocks = blocks.transpose(*order, *range(len(axes), blocks.ndim))  11.8 us
    all_to_all x1, blocking collectives, summed_on_arrival(): lax.all_to_all(blocks, axis, split_axis=0, concat_axis=0, tiled=True)  11.8 us
    dot_general x1, matrix products, shards(): jnp.dot(cotangent_full, weight, preferred_element_type=jnp.float32)  9.85 us
    dot_general x1, matrix products, shards(): lax.dot_general(cotangent_full, hidden, (((0,), (0,)), ((), ())), preferr...  9.79 us
    reduce_sum x1, other arithmetic, summed_on_arrival(): return arrived.sum(axis=0)  7.03 us
    dot_general x1, matrix products, shards(): lax.dot_general(weight, hidden, (((1,), (1,)), ((), ())), preferred_eleme...  6.95 us
  transfers between devices with their start and end apart: 3, of which 2 were waited for; matrix products, arithmetic and copies ran while one was open for 10% of the time, Pallas kernels for 0%

commit v1 on v0

v1 whole, which is shorter than its diff:
```python
import jax
import jax.numpy as jnp
from jax import lax
from jax.experimental import pallas as pl
from jax.experimental.pallas import tpu as pltpu
from jax.sharding import Mesh
from jax.sharding import PartitionSpec as P


YH, Z, YL, X, C = "yh", "z", "yl", "x", "c"
F32, F16, BF16 = jnp.float32, jnp.float16, jnp.bfloat16
VMEM = pltpu.VMEM


def turned(axis, by):
    def move(array):
        n = lax.axis_size(axis)
        return lax.ppermute(array, axis, [(i, (i + by) % n) for i in range(n)])

    return move


z_up, z_down = turned(Z, 1), turned(Z, -1)
x_up, x_down = turned(X, 1), turned(X, -1)
other_core, other_yl, other_yh = turned(C, 1), turned(YL, 1), turned(YH, 1)


def pick(array, index):
    return lax.dynamic_index_in_dim(array, index, 0, keepdims=False)


def dot(a, b, da, db):
    return lax.dot_general(a, b, (((da,), (db,)), ((), ())), preferred_element_type=F32)


def cost(flops, bytes_accessed):
    return pl.CostEstimate(flops=flops, bytes_accessed=bytes_accessed, transcendentals=0)


def out_parts(hidden, hidden_c, weight, weight_c, order):
    t, u = hidden.shape
    n, r = order.shape[0], 256

    def kernel(order_ref, h_ref, hc_ref, w_ref, wc_ref, o_ref):
        o_ref[0] = dot(h_ref[...], w_ref[...], 1, 1) + dot(hc_ref[...], wc_ref[...], 1, 1)

    rows = pl.BlockSpec((r, u), lambda i, o: (o[i], 0))
    whole = pl.BlockSpec((t, u), lambda i, o: (0, 0))
    return pl.pallas_call(
        kernel,
        grid_spec=pltpu.PrefetchScalarGridSpec(
            num_scalar_prefetch=1,
            grid=(n,),
            in_specs=[whole, whole, rows, rows],
            out_specs=pl.BlockSpec((1, t, r), lambda i, o: (i, 0, 0)),
        ),
        out_shape=jax.ShapeDtypeStruct((n, t, r), F32),
        compiler_params=pltpu.CompilerParams(vmem_limit_bytes=58 << 20),
        cost_estimate=cost(4 * n * t * r * u, 4 * n * r * u + 4 * n * t * r),
        name="out_parts",
    )(order, hidden, hidden_c, weight, weight_c)


def grad_parts(mine, theirs, hidden, hidden2):
    n, _, t, r = mine.shape
    u = hidden.shape[1]

    def kernel(a_ref, b_ref, h_ref, h2_ref, o_ref):
        for p, ref in enumerate((a_ref, b_ref)):
            o_ref[0, p] = dot(ref[0, 0], h_ref[...], 0, 0) + dot(ref[0, 1], h2_ref[...], 0, 0)

    part = pl.BlockSpec((1, 2, t, r), lambda i: (i, 0, 0, 0))
    whole = pl.BlockSpec((t, u), lambda i: (0, 0))
    return pl.pallas_call(
        kernel,
        grid=(n,),
        in_specs=[part, part, whole, whole],
        out_specs=pl.BlockSpec((1, 2, r, u), lambda i: (i, 0, 0, 0)),
        out_shape=jax.ShapeDtypeStruct((n, 2, r, u), F32),
        compiler_params=pltpu.CompilerParams(vmem_limit_bytes=20 << 20),
        cost_estimate=cost(8 * n * t * r * u, 8 * n * t * r + 8 * n * r * u),
        name="grad_parts",
    )(mine, theirs, hidden, hidden2)


def hidden_gradient(blocks, weight, order):
    t, r = blocks[0].shape[1:]
    u = weight.shape[1]
    m = len(blocks)
    n = sum(b.shape[0] for b in blocks) // 4
    assert m == 4

    def kernel(order_ref, *refs):
        cots, ws, o_ref, acc_ref = refs[:m], refs[m : 2 * m], refs[2 * m], refs[2 * m + 1]
        i = pl.program_id(0)
        total = dot(cots[0][0], ws[0][...], 1, 0)
        for a in range(1, m):
            total += dot(cots[a][0], ws[a][...], 1, 0)

        @pl.when(i == 0)
        def _():
            acc_ref[...] = total

        @pl.when(i > 0)
        def _():
            acc_ref[...] += total

        @pl.when(i == n - 1)
        def _():
            o_ref[...] = acc_ref[...].astype(BF16)

    part = pl.BlockSpec((1, t, r), lambda i, o: (i, 0, 0))
    rows = [pl.BlockSpec((r, u), lambda i, o, a=a: (o[a * n + i], 0)) for a in range(m)]
    return pl.pallas_call(
        kernel,
        grid_spec=pltpu.PrefetchScalarGridSpec(
            num_scalar_prefetch=1,
            grid=(n,),
            in_specs=[part] * m + rows,
            out_specs=pl.BlockSpec((t, u), lambda i, o: (0, 0)),
            scratch_shapes=[VMEM((t, u), F32)],
        ),
        out_shape=jax.ShapeDtypeStruct((t, u), BF16),
        compiler_params=pltpu.CompilerParams(vmem_limit_bytes=20 << 20),
        cost_estimate=cost(2 * m * n * t * r * u, 2 * m * n * (t * r + r * u)),
        name="hidden_gradient",
    )(order, *blocks, *([weight] * m))


def layer(hidden, weight, cotangent):
    tokens, units = hidden.shape
    rows = cotangent.shape[1]
    scale = float(tokens * 16) ** -0.5
    yh, z, yl, x, c = (lax.axis_index(a) for a in (YH, Z, YL, X, C))

    sib = other_yl(cotangent)
    far = lax.ppermute(cotangent, (YH, YL), [(2, 0), (1, 3)])
    near = lax.ppermute(cotangent, (YH, YL), [(2, 1), (1, 2)])
    weight_c = other_core(weight)
    hidden_c = other_core(hidden)
    hidden2 = other_yh(hidden)
    own = yl == yh
    crit0 = jnp.where(own, cotangent, sib)
    crit1 = far + near
    rest = jnp.where(own, sib, cotangent)

    c0u = x_up(crit0)
    c1d = x_down(crit1)
    c1u = x_up(crit1)
    c0d = x_down(crit0)
    c0uu = x_up(c0u)
    c1dd = x_down(c1d)
    half_t = tokens // 2
    ru = x_up(rest)
    rd = x_down(rest)
    ruu = x_up(ru[:half_t])
    rdd = x_down(rd[half_t:])

    near_x = jnp.stack([jnp.stack(p) for p in ((crit0, crit1), (c0u, c1u), (c0d, c1d))])
    near_o = other_core(near_x)
    far_x = jnp.stack([c0uu, c1dd])[None]
    far_o = other_core(far_x)
    rest_x = jnp.stack([rest, ru, rd, jnp.concatenate([ruu, rdd], 0)])
    rest_o = other_core(rest_x)

    places = [(2, 0), (2, 1), (1, 0), (1, 1), (3, 0), (3, 1)]
    order = [y * 4 + (x + k) % 4 for k, y in places] + [yl * 4 + x, (1 - yl) * 4 + x]
    order = jnp.stack([k * 2 + c for k in order]).astype(jnp.int32)
    parts = out_parts(hidden, hidden_c, weight, weight_c, order)
    up = x_up(parts[0])
    down = x_down(parts[1])
    up = x_up(jnp.stack([parts[2] + up, parts[3]]))
    down = x_down(jnp.stack([parts[4], parts[5] + down]))
    give = parts[7] + (pick(up, 1 - yl) + pick(down, 1 - yl))
    keep = parts[6] + (pick(up, yl) + pick(down, yl))
    given = other_yl(give)
    output = (keep + given).astype(BF16)

    g_near = grad_parts(near_x, near_o, hidden, hidden2)
    g_far = grad_parts(far_x, far_o, hidden, hidden2)

    def grad_part(d):
        d = d % 8
        k = (x - d // 2) % 4
        p = (d + c) % 2
        at = jnp.where(k == 3, 2, jnp.where(k == 2, 0, k))
        near_d = lax.dynamic_slice(g_near, (at, p, 0, 0), (1, 1, rows, units))[0, 0]
        return jnp.where(k == 2, pick(g_far[0], p), near_d) * 0.25

    half = rows // 2
    g = grad_part(z + 4)
    up = z_up(g[:half].astype(F16))
    down = z_down(g[half:].astype(F16))
    for k in (3, 2, 1):
        gu = grad_part(z + k)
        gd = grad_part(z - k)
        if k == 3:
            gu = jnp.concatenate([gu[:half] + up.astype(F32), gu[half:]], 0)
            gd = jnp.concatenate([gd[:half], gd[half:] + down.astype(F32)], 0)
        else:
            gu, gd = gu + up.astype(F32), gd + down.astype(F32)
        up = z_up(gu.astype(F16))
        down = z_down(gd.astype(F16))
    weight_grad = (grad_part(z) + up.astype(F32) + down.astype(F32)) * (scale * 4.0)

    crit_x = jnp.concatenate([near_x[:, 0], far_x[:, 0]], 0)
    crit_o = jnp.concatenate([near_o[:, 0], far_o[:, 0]], 0)
    order = []
    for y, cc in ((yh, c), (yh, 1 - c), (1 - yh, c), (1 - yh, 1 - c)):
        for k in (0, 1, 3, 2):
            order.append(y * 8 + (x - k) % 4 * 2 + cc)
    order = jnp.stack(order).astype(jnp.int32)
    hidden_grad = hidden_gradient([crit_x, crit_o, rest_x, rest_o], weight, order)
    return output, hidden_grad, weight_grad


def solution(mesh):
    finer = Mesh(mesh.devices.reshape(2, 8, 2, 4, 2), (YH, Z, YL, X, C))
    gx, gy = (YH, Z), (YL, X, C)
    return jax.shard_map(
        layer,
        mesh=finer,
        in_specs=(P(gx, gy), P(None, gy), P(gx, gy)),
        out_specs=(P(gx, gy), P(gx, gy), P(gx, gy)),
        check_vma=False,
    )
```

time: 286 us -> 163 us (0.57)
  waiting for transfers between devices: 146 us -> 67.4 us
  blocking collectives: 53.1 us -> 0 us
  starting transfers between devices: 4.83 us -> 45.6 us
  matrix products: 26.6 us -> 0 us
  Pallas kernels: 0 us -> 25.6 us
  local copies, waits for them, and re-layouts: 28.7 us -> 8.05 us
  between operations: 14.1 us -> 1.89 us
    reduce_scatter x2 -> x0, waiting for transfers between devices: 146 us -> none  [sum_in_order(): blocks = lax.psum_scatter(blocks, axes[k], scatter_dimension=0, tiled=True)]
    ppermute x0 -> x32, waiting for transfers between devices: none -> 67.4 us  [the longest x30 62.5 us: move(): return lax.ppermute(array, axis, [(i, (i + by) % n) for i in range(n)])]
    all_to_all x3 -> x0, blocking collectives: 53.1 us -> none  [the longest x2 41.3 us: from_everyone(): return lax.all_to_all(copies, axis, split_axis=0, concat_axis=0, tiled=True)]
    ppermute x0 -> x32, starting transfers between devices: none -> 45.6 us  [the longest x30 43.6 us: move(): return lax.ppermute(array, axis, [(i, (i + by) % n) for i in range(n)])]
    dot_general x3 -> x0, matrix products: 26.6 us -> none  [the longest x1 9.85 us: shards(): jnp.dot(cotangent_full, weight, preferred_element_type=jnp.float32)]
    pallas_call x0 -> x4, Pallas kernels: none -> 25.6 us  [the longest x1 11.1 us: out_parts(): pl.pallas_call(kernel, grid_spec=pltpu.PrefetchScalarGridSpec(num_scalar_...]
    transpose x2 -> x0, local copies, waits for them, and re-layouts: 18.2 us -> none  [the longest x1 11.8 us: sum_in_order(): blocks = blocks.transpose(*order, *range(len(axes), blocks.ndim))]
    reduce_sum x2 -> x0, other arithmetic: 9.72 us -> none  [the longest x1 7.03 us: summed_on_arrival(): return arrived.sum(axis=0)]
  transfers between devices with their start and end apart: 3 -> 32, of which waited for: 2 -> 16; matrix products, arithmetic and copies ran while one was open for 10% -> 11% of each run, Pallas kernels for 0% -> 16%
where the time goes in v1:
time: 163 us; the launch traced here: 162 us
  waiting for transfers between devices  67.4 us (41%)
  starting transfers between devices  45.6 us (28%)
  Pallas kernels  25.6 us (16%)
  other arithmetic  13.6 us (8%)
  local copies, waits for them, and re-layouts  8.05 us (5%)
  between operations  1.89 us (1%)
    ppermute x30, waiting for transfers between devices, move(): return lax.ppermute(array, axis, [(i, (i + by) % n) for i in range(n)])  62.5 us
    ppermute x30, starting transfers between devices, move(): return lax.ppermute(array, axis, [(i, (i + by) % n) for i in range(n)])  43.6 us
    pallas_call x1, Pallas kernels, out_parts(): pl.pallas_call(kernel, grid_spec=pltpu.PrefetchScalarGridSpec(num_scalar_...  11.1 us
    pallas_call x1, Pallas kernels, hidden_gradient(): pl.pallas_call(kernel, grid_spec=pltpu.PrefetchScalarGridSpec(num_scalar_...  8.22 us
    pallas_call x2, Pallas kernels, grad_parts(): pl.pallas_call(kernel, grid=(n,), in_specs=[part, part, whole, whole], ou...  6.2 us
    ppermute x1, waiting for transfers between devices, layer(): far = lax.ppermute(cotangent, (YH, YL), [(2, 0), (1, 3)])  4.86 us
  transfers between devices with their start and end apart: 32, of which 16 were waited for; matrix products, arithmetic and copies ran while one was open for 11% of the time, Pallas kernels for 16%

profile of v1, /device:TPU:1, one launch (start us, length us, event | category | flops | bytes accessed | tf_op | source)
XLA Modules:
  0.0 162.0 jit_solution(12259426024530531937)
XLA Ops:
  0.6 3.3 %collective-permute-start.1 = (bf16[4096,896]{1,0:T(8,128)(2,1)}, bf16[4096,896]{1,0:T(8,128)(2,1)}, u32[]{:S(2)}, u32[]{:S(2)}) collective-permute-start(bf16[4096,896]{1,0:T(8,128)(2,1)} %refs_7_.1), channel_id=1, source_target_pairs={{0,1},{1,0},{2,3},{3,2},{4,5},{5,4},{6,7},{7,6},{8,9},{9,8},{10,11... | collective-permute-start | bytes 22020104 | tf_op jit(solution)/shard_map/ppermute | solution.py:18
  3.9 1.3 collective-permute-start.8
  5.2 0.7 collective-permute-start.9
  5.9 4.6 %collective-permute-start.7 = (bf16[512,256]{1,0:T(8,128)(2,1)}, bf16[512,256]{1,0:T(8,128)(2,1)S(1)}, u32[]{:S(2)}, u32[]{:S(2)}) collective-permute-start(bf16[512,256]{1,0:T(8,128)(2,1)} %param.5), channel_id=1, source_target_pairs={{0,8},{8,0},{1,9},{9,1},{2,10},{10,2},{3,11},{11,3},{4,12},{12,4},... | collective-permute-start | bytes 786440 | tf_op jit(solution)/shard_map/ppermute | solution.py:18
  10.5 4.9 %collective-permute-done.8 = bf16[512,256]{1,0:T(8,128)(2,1)S(1)} collective-permute-done((bf16[512,256]{1,0:T(8,128)(2,1)}, bf16[512,256]{1,0:T(8,128)(2,1)S(1)}, u32[]{:S(2)}, u32[]{:S(2)}) %collective-permute-start.8) | collective-permute-done | bytes 262176 | tf_op jit(solution)/shard_map/ppermute | solution.py:137
  15.4 0.8 collective-permute-start.13
  16.3 3.3 %collective-permute-done.7 = bf16[512,256]{1,0:T(8,128)(2,1)S(1)} collective-permute-done((bf16[512,256]{1,0:T(8,128)(2,1)}, bf16[512,256]{1,0:T(8,128)(2,1)S(1)}, u32[]{:S(2)}, u32[]{:S(2)}) %collective-permute-start.7) | collective-permute-done | bytes 262176 | tf_op jit(solution)/shard_map/ppermute | solution.py:18
  19.6 1.0 broadcast_select_fusion
  20.6 2.6 %collective-permute-start.12 = (bf16[512,256]{1,0:T(8,128)(2,1)S(1)}, bf16[512,256]{1,0:T(8,128)(2,1)S(1)}, u32[]{:S(2)}, u32[]{:S(2)}) collective-permute-start(bf16[512,256]{1,0:T(8,128)(2,1)S(1)} %get-tuple-element.15), channel_id=1, source_target_pairs={{0,6},{2,0},{4,2},{6,4},{1,7},{3,1},{5,3},{7,5},{8,14},{10,8},{12,... | collective-permute-start | bytes 786440 | tf_op jit(solution)/shard_map/ppermute | solution.py:18
  23.2 0.2 collective-permute-start.11
  23.4 2.6 %collective-permute-start.19 = (bf16[512,256]{1,0:T(8,128)(2,1)S(1)}, bf16[512,256]{1,0:T(8,128)(2,1)S(1)}, u32[]{:S(2)}, u32[]{:S(2)}) collective-permute-start(bf16[512,256]{1,0:T(8,128)(2,1)S(1)} %get-tuple-element.14), channel_id=1, source_target_pairs={{0,6},{2,0},{4,2},{6,4},{1,7},{3,1},{5,3},{7,5},{8,14},{10,8},{12,... | collective-permute-start | bytes 786440 | tf_op jit(solution)/shard_map/ppermute | solution.py:18
  26.0 2.5 %collective-permute-done.12 = bf16[512,256]{1,0:T(8,128)(2,1)S(1)} collective-permute-done((bf16[512,256]{1,0:T(8,128)(2,1)S(1)}, bf16[512,256]{1,0:T(8,128)(2,1)S(1)}, u32[]{:S(2)}, u32[]{:S(2)}) %collective-permute-start.12) | collective-permute-done | bytes 262176 | tf_op jit(solution)/shard_map/ppermute | solution.py:18
  28.6 2.6 %collective-permute-done.10 = bf16[512,256]{1,0:T(8,128)(2,1)} collective-permute-done((bf16[512,256]{1,0:T(8,128)(2,1)S(1)}, bf16[512,256]{1,0:T(8,128)(2,1)}, u32[]{:S(2)}, u32[]{:S(2)}) %collective-permute-start.10) | collective-permute-done | bytes 262176 | tf_op jit(solution)/shard_map/ppermute | solution.py:18
  31.2 5.5 %collective-permute-done.11 = bf16[512,256]{1,0:T(8,128)(2,1)S(1)} collective-permute-done((bf16[512,256]{1,0:T(8,128)(2,1)S(1)}, bf16[512,256]{1,0:T(8,128)(2,1)S(1)}, u32[]{:S(2)}, u32[]{:S(2)}) %collective-permute-start.11) | collective-permute-done | bytes 262176 | tf_op jit(solution)/shard_map/ppermute | solution.py:18
  36.7 1.0 maximum_bitcast_fusion.1
  37.7 0.2 pad_maximum_fusion.a_ref
  37.9 2.1 %collective-permute-start.16 = (bf16[3,2,512,256]{3,2,1,0:T(8,128)(2,1)S(1)}, bf16[3,2,512,256]{3,2,1,0:T(8,128)(2,1)}, u32[]{:S(2)}, u32[]{:S(2)}) collective-permute-start(bf16[3,2,512,256]{3,2,1,0:T(8,128)(2,1)S(1)} %pad_maximum_fusion.a_ref), channel_id=1, source_target_pairs={{0,1},{1,0},{2,3},{3,2},{4,5},{5,4},{6,7},{7,6},{8,9},{9,8},{10,11... | collective-permute-start | bytes 4718600 | tf_op jit(solution)/shard_map/ppermute | solution.py:18
  40.0 2.7 %collective-permute-start.15 = (bf16[512,256]{1,0:T(8,128)(2,1)S(1)}, bf16[512,256]{1,0:T(8,128)(2,1)}, u32[]{:S(2)}, u32[]{:S(2)}) collective-permute-start(bf16[512,256]{1,0:T(8,128)(2,1)S(1)} %collective-permute-done.13), channel_id=1, source_target_pairs={{0,6},{2,0},{4,2},{6,4},{1,7},{3,1},{5,3},{7,5},{8,14},{10,8},{12,... | collective-permute-start | bytes 786440 | tf_op jit(solution)/shard_map/ppermute | solution.py:18
  43.5 0.7 stack.161.order_ref
  44.3 4.7 %collective-permute-done.18 = bf16[512,256]{1,0:T(8,128)(2,1)S(1)} collective-permute-done((bf16[512,256]{1,0:T(8,128)(2,1)S(1)}, bf16[512,256]{1,0:T(8,128)(2,1)S(1)}, u32[]{:S(2)}, u32[]{:S(2)}) %collective-permute-start.18) | collective-permute-done | bytes 262176 | tf_op jit(solution)/shard_map/ppermute | solution.py:18
  49.0 2.5 %collective-permute-start.21 = (bf16[256,256]{1,0:T(8,128)(2,1)S(1)}, bf16[256,256]{1,0:T(8,128)(2,1)S(1)}, u32[]{:S(2)}, u32[]{:S(2)}) collective-permute-start(bf16[256,256]{1,0:T(8,128)(2,1)S(1)} %slice.115), channel_id=1, source_target_pairs={{0,6},{2,0},{4,2},{6,4},{1,7},{3,1},{5,3},{7,5},{8,14},{10,8},{12,... | collective-permute-start | bytes 393224 | tf_op jit(solution)/shard_map/ppermute | solution.py:18
  51.5 3.2 %collective-permute-done.14 = bf16[512,256]{1,0:T(8,128)(2,1)} collective-permute-done((bf16[512,256]{1,0:T(8,128)(2,1)}, bf16[512,256]{1,0:T(8,128)(2,1)}, u32[]{:S(2)}, u32[]{:S(2)}) %collective-permute-start.14) | collective-permute-done | bytes 262176 | tf_op jit(solution)/shard_map/ppermute | solution.py:18
  54.8 1.1 maximum_bitcast_fusion.3.a_ref
  55.9 1.0 collective-permute-start
  56.9 3.1 %collective-permute-done.20 = bf16[256,256]{1,0:T(8,128)(2,1)S(1)} collective-permute-done((bf16[256,256]{1,0:T(8,128)(2,1)S(1)}, bf16[256,256]{1,0:T(8,128)(2,1)S(1)}, u32[]{:S(2)}, u32[]{:S(2)}) %collective-permute-start.20) | collective-permute-done | bytes 131104 | tf_op jit(solution)/shard_map/ppermute | solution.py:18
  60.0 1.8 %collective-permute-start.17 = (bf16[1,2,512,256]{3,2,1,0:T(8,128)(2,1)S(1)}, bf16[1,2,512,256]{3,2,1,0:T(8,128)(2,1)S(1)}, u32[]{:S(2)}, u32[]{:S(2)}) collective-permute-start(bf16[1,2,512,256]{3,2,1,0:T(8,128)(2,1)S(1)} %maximum_bitcast_fusion.3.a_ref), channel_id=1, source_target_pairs={{0,1},{1,0},{2,3},{3,2},{4,5},{5,4},{6,7},{7,6},{8,9},{9,8},{10,11... | collective-permute-start | bytes 1572872 | tf_op jit(solution)/shard_map/ppermute | solution.py:18
  61.9 1.2 pad_maximum_fusion.5.refs_2_
  63.1 1.1 pad_maximum_fusion.3.refs_0_
  64.2 6.7 %collective-permute-done.23.h2_ref = bf16[512,896]{1,0:T(8,128)(2,1)S(1)} collective-permute-done((bf16[512,896]{1,0:T(8,128)(2,1)S(1)}, bf16[512,896]{1,0:T(8,128)(2,1)S(1)}, u32[]{:S(2)}, u32[]{:S(2)}) %collective-permute-start.23) | collective-permute-done | bytes 917536 | tf_op jit(solution)/shard_map/ppermute | solution.py:18
  70.9 2.4 %collective-permute-start.22 = (bf16[4,512,256]{2,1,0:T(8,128)(2,1)S(1)}, bf16[4,512,256]{2,1,0:T(8,128)(2,1)}, u32[]{:S(2)}, u32[]{:S(2)}) collective-permute-start(bf16[4,512,256]{2,1,0:T(8,128)(2,1)S(1)} %pad_maximum_fusion.5.refs_2_), channel_id=1, source_target_pairs={{0,1},{1,0},{2,3},{3,2},{4,5},{5,4},{6,7},{7,6},{8,9},{9,8},{10,11... | collective-permute-start | bytes 3145736 | tf_op jit(solution)/shard_map/ppermute | solution.py:18
  73.3 1.3 grad_parts.2
  74.6 4.9 %grad_parts.3 = f32[3,2,256,896]{3,2,1,0:T(8,128)S(1)} custom-call(bf16[3,2,512,256]{3,2,1,0:T(8,128)(2,1)S(1)} %pad_maximum_fusion.a_ref, bf16[3,2,512,256]{3,2,1,0:T(8,128)(2,1)} %collective-permute-done.16.b_ref, bf16[512,896]{1,0:T(8,128)(2,1)S(1)} %copy-done.1, bf16[512,896]{1,0:T(8,128)(2,1)S(1)} %collective-permute-done.23.h2_ref), custom_call_target="tpu_custom_call" | custom-call | flops 2818572288 | bytes 8650752 | tf_op jit(solution)/shard_map/grad_parts/pallas_call | solution.py:74
  79.5 0.3 select_multiply_fusion.1
  79.8 2.2 %copy-done = f32[3,2,256,896]{3,2,1,0:T(8,128)} copy-done((f32[3,2,256,896]{3,2,1,0:T(8,128)}, f32[3,2,256,896]{3,2,1,0:T(8,128)S(1)}, u32[]{:S(2)}) %copy-start) | copy-done | bytes 5505048
  82.0 0.8 slice_bitcast_fusion.11
  82.7 1.6 %collective-permute-start.24 = (f16[128,896]{1,0:T(8,128)(2,1)S(1)}, f16[128,896]{1,0:T(8,128)(2,1)S(1)}, u32[]{:S(2)}, u32[]{:S(2)}) collective-permute-start(f16[128,896]{1,0:T(8,128)(2,1)S(1)} %get-tuple-element.16), channel_id=1, source_target_pairs={{0,16},{16,32},{32,48},{48,64},{64,80},{80,96},{96,112},{112,0},{1... | collective-permute-start | bytes 688136 | tf_op jit(solution)/shard_map/ppermute | solution.py:18
  84.4 3.9 %collective-permute-start.28 = (f16[128,896]{1,0:T(8,128)(2,1)}, f16[128,896]{1,0:T(8,128)(2,1)}, u32[]{:S(2)}, u32[]{:S(2)}) collective-permute-start(f16[128,896]{1,0:T(8,128)(2,1)} %get-tuple-element.17), channel_id=1, source_target_pairs={{0,112},{16,0},{32,16},{48,32},{64,48},{80,64},{96,80},{112,96},{1... | collective-permute-start | bytes 688136 | tf_op jit(solution)/shard_map/ppermute | solution.py:18
  88.3 0.7 fusion.19
  89.1 5.2 %collective-permute-done.24 = f16[128,896]{1,0:T(8,128)(2,1)S(1)} collective-permute-done((f16[128,896]{1,0:T(8,128)(2,1)S(1)}, f16[128,896]{1,0:T(8,128)(2,1)S(1)}, u32[]{:S(2)}, u32[]{:S(2)}) %collective-permute-start.24) | collective-permute-done | bytes 229408 | tf_op jit(solution)/shard_map/ppermute | solution.py:18
  94.4 0.9 pad_maximum_fusion.6
  95.3 0.9 copy-done.9
  96.2 11.1 %out_parts.1 = f32[8,512,256]{2,1,0:T(8,128)} custom-call(s32[8]{0:T(128)} %stack.161.order_ref, bf16[512,896]{1,0:T(8,128)(2,1)} %h_ref.5, bf16[512,896]{1,0:T(8,128)(2,1)} %copy-done.9, bf16[4096,896]{1,0:T(8,128)(2,1)} %refs_7_.1, bf16[4096,896]{1,0:T(8,128)(2,1)} %collective-permute-done.1.wc_ref), custom_call_target="tpu_custom_call" | custom-call | flops 3758096384 | bytes 11534336 | tf_op jit(solution)/shard_map/out_parts/pallas_call | solution.py:49
  107.3 1.8 %slice_bitcast_fusion.4 = (f32[512,256]{1,0:T(8,128)S(1)}, f32[512,256]{1,0:T(8,128)S(1)}, f32[1,512,256]{2,1,0:T(8,128)S(1)}, f32[1,512,256]{2,1,0:T(8,128)S(1)}) fusion(f32[8,512,256]{2,1,0:T(8,128)} %out_parts.1), kind=kLoop, calls=%fused_computation.28 | loop fusion | bytes 4194304 | tf_op jit(solution)/shard_map/squeeze | solution.py:170
  109.2 2.7 %collective-permute-start.4 = (f32[512,256]{1,0:T(8,128)S(1)}, f32[512,256]{1,0:T(8,128)S(1)}, u32[]{:S(2)}, u32[]{:S(2)}) collective-permute-start(f32[512,256]{1,0:T(8,128)S(1)} %get-tuple-element.11), channel_id=1, source_target_pairs={{0,6},{2,0},{4,2},{6,4},{1,7},{3,1},{5,3},{7,5},{8,14},{10,8},{12,... | collective-permute-start | bytes 1572872 | tf_op jit(solution)/shard_map/ppermute | solution.py:18
  111.9 1.1 fusion.15
  113.2 2.8 %collective-permute-start.29 = (f16[256,896]{1,0:T(8,128)(2,1)S(1)}, f16[256,896]{1,0:T(8,128)(2,1)S(1)}, u32[]{:S(2)}, u32[]{:S(2)}) collective-permute-start(f16[256,896]{1,0:T(8,128)(2,1)S(1)} %pad_maximum_fusion.7), channel_id=1, source_target_pairs={{0,112},{16,0},{32,16},{48,32},{64,48},{80,64},{96,80},{112,96},{1... | collective-permute-start | bytes 1376264 | tf_op jit(solution)/shard_map/ppermute | solution.py:18
  115.9 1.5 fusion.2
  117.5 5.8 %collective-permute-done.2 = f32[512,256]{1,0:T(8,128)S(1)} collective-permute-done((f32[512,256]{1,0:T(8,128)S(1)}, f32[512,256]{1,0:T(8,128)S(1)}, u32[]{:S(2)}, u32[]{:S(2)}) %collective-permute-start.2) | collective-permute-done | bytes 524320 | tf_op jit(solution)/shard_map/ppermute | solution.py:18
  123.3 0.2 fusion.10
  123.6 2.5 %collective-permute-start.5 = (f32[2,512,256]{2,1,0:T(8,128)S(1)}, f32[2,512,256]{2,1,0:T(8,128)S(1)}, u32[]{:S(2)}, u32[]{:S(2)}) collective-permute-start(f32[2,512,256]{2,1,0:T(8,128)S(1)} %pad_maximum_fusion.2), channel_id=1, source_target_pairs={{0,6},{2,0},{4,2},{6,4},{1,7},{3,1},{5,3},{7,5},{8,14},{10,8},{12,... | collective-permute-start | bytes 3145736 | tf_op jit(solution)/shard_map/ppermute | solution.py:18
  126.1 0.3 collective-permute-start.3
  126.5 2.6 %collective-permute-done.26 = f16[256,896]{1,0:T(8,128)(2,1)S(1)} collective-permute-done((f16[256,896]{1,0:T(8,128)(2,1)S(1)}, f16[256,896]{1,0:T(8,128)(2,1)S(1)}, u32[]{:S(2)}, u32[]{:S(2)}) %collective-permute-start.26) | collective-permute-done | bytes 458784 | tf_op jit(solution)/shard_map/ppermute | solution.py:18
  129.1 0.4 fusion.3
  129.7 1.5 slice_bitcast_fusion
  131.2 1.4 collective-permute-start.27
  132.6 6.5 %collective-permute-done.30 = f16[256,896]{1,0:T(8,128)(2,1)S(1)} collective-permute-done((f16[256,896]{1,0:T(8,128)(2,1)S(1)}, f16[256,896]{1,0:T(8,128)(2,1)S(1)}, u32[]{:S(2)}, u32[]{:S(2)}) %collective-permute-start.30) | collective-permute-done | bytes 458784 | tf_op jit(solution)/shard_map/ppermute | solution.py:18
  139.1 0.2 fusion.1
  139.3 1.6 collective-permute-start.31
  140.9 6.0 %collective-permute-done.5 = f32[2,512,256]{2,1,0:T(8,128)S(1)} collective-permute-done((f32[2,512,256]{2,1,0:T(8,128)S(1)}, f32[2,512,256]{2,1,0:T(8,128)S(1)}, u32[]{:S(2)}, u32[]{:S(2)}) %collective-permute-start.5) | collective-permute-done | bytes 1048608 | tf_op jit(solution)/shard_map/ppermute | solution.py:18
  146.9 3.4 %collective-permute-done.3 = f32[2,512,256]{2,1,0:T(8,128)S(1)} collective-permute-done((f32[2,512,256]{2,1,0:T(8,128)S(1)}, f32[2,512,256]{2,1,0:T(8,128)S(1)}, u32[]{:S(2)}, u32[]{:S(2)}) %collective-permute-start.3) | collective-permute-done | bytes 1048608 | tf_op jit(solution)/shard_map/ppermute | solution.py:18
  150.6 8.2 %hidden_gradient.1 = bf16[512,896]{1,0:T(8,128)(2,1)} custom-call(s32[16]{0:T(128)S(1)} %stack.182.order_ref, bf16[4,512,256]{2,1,0:T(8,128)(2,1)S(1)} %copy-done.2, bf16[4,512,256]{2,1,0:T(8,128)(2,1)S(1)} %pad_maximum_fusion.4.refs_1_, bf16[4,512,256]{2,1,0:T(8,128)(2,1)S(1)} %pad_maximum_fusion.5.refs_2_, ...), custom_call_target="tpu_custom_call" | custom-call | flops 3758096384 | bytes 11534336 | tf_op jit(solution)/shard_map/hidden_gradient/pallas_call | solution.py:114
  158.8 1.2 fusion.5
  160.0 1.2 collective-permute-done.6
  161.2 0.8 fusion.13
  (75 shorter events, 1.4 us)
Async XLA Ops:
  0.6 95.6 %collective-permute-start.1 = (bf16[4096,896]{1,0:T(8,128)(2,1)}, bf16[4096,896]{1,0:T(8,128)(2,1)}, u32[]{:S(2)}, u32[]{:S(2)}) collective-permute-start(bf16[4096,896]{1,0:T(8,128)(2,1)} %refs_7_.1), channel_id=1, source_target_pairs={{0,1},{1,0},{2,3},{3,2},{4,5},{5,4},{6,7},{7,6},{8,9},{9,8},{10,11... | collective-permute-start | bytes 22020104 | tf_op jit(solution)/shard_map/ppermute | solution.py:18
  3.9 11.4 %collective-permute-start.8 = (bf16[512,256]{1,0:T(8,128)(2,1)}, bf16[512,256]{1,0:T(8,128)(2,1)S(1)}, u32[]{:S(2)}, u32[]{:S(2)}) collective-permute-start(bf16[512,256]{1,0:T(8,128)(2,1)} %param.5), channel_id=1, source_target_pairs={{128,0},{8,136},{129,1},{9,137},{130,2},{10,138},{131,3},{11,139},... | collective-permute-start | bytes 786440 | tf_op jit(solution)/shard_map/ppermute | solution.py:137
  5.2 10.1 %collective-permute-start.9 = (bf16[512,256]{1,0:T(8,128)(2,1)}, bf16[512,256]{1,0:T(8,128)(2,1)S(1)}, u32[]{:S(2)}, u32[]{:S(2)}) collective-permute-start(bf16[512,256]{1,0:T(8,128)(2,1)} %param.5), channel_id=1, source_target_pairs={{128,8},{8,128},{129,9},{9,129},{130,10},{10,130},{131,11},{11,131... | collective-permute-start | bytes 786440 | tf_op jit(solution)/shard_map/ppermute | solution.py:138
  5.9 13.7 %collective-permute-start.7 = (bf16[512,256]{1,0:T(8,128)(2,1)}, bf16[512,256]{1,0:T(8,128)(2,1)S(1)}, u32[]{:S(2)}, u32[]{:S(2)}) collective-permute-start(bf16[512,256]{1,0:T(8,128)(2,1)} %param.5), channel_id=1, source_target_pairs={{0,8},{8,0},{1,9},{9,1},{2,10},{10,2},{3,11},{11,3},{4,12},{12,4},... | collective-permute-start | bytes 786440 | tf_op jit(solution)/shard_map/ppermute | solution.py:18
  15.4 8.0 %collective-permute-start.13 = (bf16[512,256]{1,0:T(8,128)(2,1)S(1)}, bf16[512,256]{1,0:T(8,128)(2,1)S(1)}, u32[]{:S(2)}, u32[]{:S(2)}) collective-permute-start(bf16[512,256]{1,0:T(8,128)(2,1)S(1)} %add.471), channel_id=1, source_target_pairs={{0,6},{2,0},{4,2},{6,4},{1,7},{3,1},{5,3},{7,5},{8,14},{10,8},{12,... | collective-permute-start | bytes 786440 | tf_op jit(solution)/shard_map/ppermute | solution.py:18
  20.6 19.4 %copy-start.6 = (bf16[512,256]{1,0:T(8,128)(2,1)}, bf16[512,256]{1,0:T(8,128)(2,1)S(1)}, u32[]{:S(2)}) copy-start(bf16[512,256]{1,0:T(8,128)(2,1)S(1)} %get-tuple-element.14) | copy-start | bytes 786436
  20.6 7.9 %collective-permute-start.12 = (bf16[512,256]{1,0:T(8,128)(2,1)S(1)}, bf16[512,256]{1,0:T(8,128)(2,1)S(1)}, u32[]{:S(2)}, u32[]{:S(2)}) collective-permute-start(bf16[512,256]{1,0:T(8,128)(2,1)S(1)} %get-tuple-element.15), channel_id=1, source_target_pairs={{0,6},{2,0},{4,2},{6,4},{1,7},{3,1},{5,3},{7,5},{8,14},{10,8},{12,... | collective-permute-start | bytes 786440 | tf_op jit(solution)/shard_map/ppermute | solution.py:18
  23.2 8.0 %collective-permute-start.10 = (bf16[512,256]{1,0:T(8,128)(2,1)S(1)}, bf16[512,256]{1,0:T(8,128)(2,1)}, u32[]{:S(2)}, u32[]{:S(2)}) collective-permute-start(bf16[512,256]{1,0:T(8,128)(2,1)S(1)} %get-tuple-element.15), channel_id=1, source_target_pairs={{0,2},{2,4},{4,6},{6,0},{1,3},{3,5},{5,7},{7,1},{8,10},{10,12},{12... | collective-permute-start | bytes 786440 | tf_op jit(solution)/shard_map/ppermute | solution.py:18
  23.2 13.5 %collective-permute-start.11 = (bf16[512,256]{1,0:T(8,128)(2,1)S(1)}, bf16[512,256]{1,0:T(8,128)(2,1)S(1)}, u32[]{:S(2)}, u32[]{:S(2)}) collective-permute-start(bf16[512,256]{1,0:T(8,128)(2,1)S(1)} %add.471), channel_id=1, source_target_pairs={{0,2},{2,4},{4,6},{6,0},{1,3},{3,5},{5,7},{7,1},{8,10},{10,12},{12... | collective-permute-start | bytes 786440 | tf_op jit(solution)/shard_map/ppermute | solution.py:18
  23.4 19.3 %collective-permute-start.19 = (bf16[512,256]{1,0:T(8,128)(2,1)S(1)}, bf16[512,256]{1,0:T(8,128)(2,1)S(1)}, u32[]{:S(2)}, u32[]{:S(2)}) collective-permute-start(bf16[512,256]{1,0:T(8,128)(2,1)S(1)} %get-tuple-element.14), channel_id=1, source_target_pairs={{0,6},{2,0},{4,2},{6,4},{1,7},{3,1},{5,3},{7,5},{8,14},{10,8},{12,... | collective-permute-start | bytes 786440 | tf_op jit(solution)/shard_map/ppermute | solution.py:18
  37.7 11.3 %copy-start.1 = (bf16[512,896]{1,0:T(8,128)(2,1)S(1)}, bf16[512,896]{1,0:T(8,128)(2,1)}, u32[]{:S(2)}) copy-start(bf16[512,896]{1,0:T(8,128)(2,1)} %h_ref.5) | copy-start | bytes 2752516
  37.9 36.7 %collective-permute-start.16 = (bf16[3,2,512,256]{3,2,1,0:T(8,128)(2,1)S(1)}, bf16[3,2,512,256]{3,2,1,0:T(8,128)(2,1)}, u32[]{:S(2)}, u32[]{:S(2)}) collective-permute-start(bf16[3,2,512,256]{3,2,1,0:T(8,128)(2,1)S(1)} %pad_maximum_fusion.a_ref), channel_id=1, source_target_pairs={{0,1},{1,0},{2,3},{3,2},{4,5},{5,4},{6,7},{7,6},{8,9},{9,8},{10,11... | collective-permute-start | bytes 4718600 | tf_op jit(solution)/shard_map/ppermute | solution.py:18
  40.0 9.0 %collective-permute-start.18 = (bf16[512,256]{1,0:T(8,128)(2,1)S(1)}, bf16[512,256]{1,0:T(8,128)(2,1)S(1)}, u32[]{:S(2)}, u32[]{:S(2)}) collective-permute-start(bf16[512,256]{1,0:T(8,128)(2,1)S(1)} %get-tuple-element.14), channel_id=1, source_target_pairs={{0,2},{2,4},{4,6},{6,0},{1,3},{3,5},{5,7},{7,1},{8,10},{10,12},{12... | collective-permute-start | bytes 786440 | tf_op jit(solution)/shard_map/ppermute | solution.py:18
  40.0 9.0 %collective-permute-start.15 = (bf16[512,256]{1,0:T(8,128)(2,1)S(1)}, bf16[512,256]{1,0:T(8,128)(2,1)}, u32[]{:S(2)}, u32[]{:S(2)}) collective-permute-start(bf16[512,256]{1,0:T(8,128)(2,1)S(1)} %collective-permute-done.13), channel_id=1, source_target_pairs={{0,6},{2,0},{4,2},{6,4},{1,7},{3,1},{5,3},{7,5},{8,14},{10,8},{12,... | collective-permute-start | bytes 786440 | tf_op jit(solution)/shard_map/ppermute | solution.py:18
  42.7 19.2 %copy-start.10 = (bf16[512,256]{1,0:T(8,128)(2,1)}, bf16[512,256]{1,0:T(8,128)(2,1)S(1)}, u32[]{:S(2)}) copy-start(bf16[512,256]{1,0:T(8,128)(2,1)S(1)} %collective-permute-done.19) | copy-start | bytes 786436
  42.7 12.0 %collective-permute-start.14 = (bf16[512,256]{1,0:T(8,128)(2,1)}, bf16[512,256]{1,0:T(8,128)(2,1)}, u32[]{:S(2)}, u32[]{:S(2)}) collective-permute-start(bf16[512,256]{1,0:T(8,128)(2,1)} %collective-permute-done.10), channel_id=1, source_target_pairs={{0,2},{2,4},{4,6},{6,0},{1,3},{3,5},{5,7},{7,1},{8,10},{10,12},{12... | collective-permute-start | bytes 786440 | tf_op jit(solution)/shard_map/ppermute | solution.py:18
  44.2 17.6 %copy-start.7 = (bf16[512,256]{1,0:T(8,128)(2,1)S(1)}, bf16[512,256]{1,0:T(8,128)(2,1)}, u32[]{:S(2)}) copy-start(bf16[512,256]{1,0:T(8,128)(2,1)} %copy-done.6) | copy-start | bytes 786436
  49.0 12.9 %copy-start.11 = (bf16[512,256]{1,0:T(8,128)(2,1)}, bf16[512,256]{1,0:T(8,128)(2,1)S(1)}, u32[]{:S(2)}) copy-start(bf16[512,256]{1,0:T(8,128)(2,1)S(1)} %collective-permute-done.18) | copy-start | bytes 786436
  49.0 21.9 %collective-permute-start.23 = (bf16[512,896]{1,0:T(8,128)(2,1)S(1)}, bf16[512,896]{1,0:T(8,128)(2,1)S(1)}, u32[]{:S(2)}, u32[]{:S(2)}) collective-permute-start(bf16[512,896]{1,0:T(8,128)(2,1)S(1)} %copy-done.1), channel_id=1, source_target_pairs={{0,128},{128,0},{1,129},{129,1},{2,130},{130,2},{3,131},{131,3},{4... | collective-permute-start | bytes 2752520 | tf_op jit(solution)/shard_map/ppermute | solution.py:18
  49.0 6.8 %collective-permute-start.21 = (bf16[256,256]{1,0:T(8,128)(2,1)S(1)}, bf16[256,256]{1,0:T(8,128)(2,1)S(1)}, u32[]{:S(2)}, u32[]{:S(2)}) collective-permute-start(bf16[256,256]{1,0:T(8,128)(2,1)S(1)} %slice.115), channel_id=1, source_target_pairs={{0,6},{2,0},{4,2},{6,4},{1,7},{3,1},{5,3},{7,5},{8,14},{10,8},{12,... | collective-permute-start | bytes 393224 | tf_op jit(solution)/shard_map/ppermute | solution.py:18
  54.7 5.3 %collective-permute-start.20 = (bf16[256,256]{1,0:T(8,128)(2,1)S(1)}, bf16[256,256]{1,0:T(8,128)(2,1)S(1)}, u32[]{:S(2)}, u32[]{:S(2)}) collective-permute-start(bf16[256,256]{1,0:T(8,128)(2,1)S(1)} %slice.114), channel_id=1, source_target_pairs={{0,2},{2,4},{4,6},{6,0},{1,3},{3,5},{5,7},{7,1},{8,10},{10,12},{12... | collective-permute-start | bytes 393224 | tf_op jit(solution)/shard_map/ppermute | solution.py:18
  55.9 39.4 %collective-permute-start = (bf16[512,896]{1,0:T(8,128)(2,1)S(1)}, bf16[512,896]{1,0:T(8,128)(2,1)S(1)}, u32[]{:S(2)}, u32[]{:S(2)}) collective-permute-start(bf16[512,896]{1,0:T(8,128)(2,1)S(1)} %copy-done.1), channel_id=1, source_target_pairs={{0,1},{1,0},{2,3},{3,2},{4,5},{5,4},{6,7},{7,6},{8,9},{9,8},{10,11... | collective-permute-start | bytes 2752520 | tf_op jit(solution)/shard_map/ppermute | solution.py:18
  60.0 13.2 %collective-permute-start.17 = (bf16[1,2,512,256]{3,2,1,0:T(8,128)(2,1)S(1)}, bf16[1,2,512,256]{3,2,1,0:T(8,128)(2,1)S(1)}, u32[]{:S(2)}, u32[]{:S(2)}) collective-permute-start(bf16[1,2,512,256]{3,2,1,0:T(8,128)(2,1)S(1)} %maximum_bitcast_fusion.3.a_ref), channel_id=1, source_target_pairs={{0,1},{1,0},{2,3},{3,2},{4,5},{5,4},{6,7},{7,6},{8,9},{9,8},{10,11... | collective-permute-start | bytes 1572872 | tf_op jit(solution)/shard_map/ppermute | solution.py:18
  70.9 79.7 %collective-permute-start.22 = (bf16[4,512,256]{2,1,0:T(8,128)(2,1)S(1)}, bf16[4,512,256]{2,1,0:T(8,128)(2,1)}, u32[]{:S(2)}, u32[]{:S(2)}) collective-permute-start(bf16[4,512,256]{2,1,0:T(8,128)(2,1)S(1)} %pad_maximum_fusion.5.refs_2_), channel_id=1, source_target_pairs={{0,1},{1,0},{2,3},{3,2},{4,5},{5,4},{6,7},{7,6},{8,9},{9,8},{10,11... | collective-permute-start | bytes 3145736 | tf_op jit(solution)/shard_map/ppermute | solution.py:18
  73.3 1.3 copy-start.3
  79.5 2.5 %copy-start = (f32[3,2,256,896]{3,2,1,0:T(8,128)}, f32[3,2,256,896]{3,2,1,0:T(8,128)S(1)}, u32[]{:S(2)}) copy-start(f32[3,2,256,896]{3,2,1,0:T(8,128)S(1)} %grad_parts.3) | copy-start | bytes 16515076
  82.7 11.5 %collective-permute-start.24 = (f16[128,896]{1,0:T(8,128)(2,1)S(1)}, f16[128,896]{1,0:T(8,128)(2,1)S(1)}, u32[]{:S(2)}, u32[]{:S(2)}) collective-permute-start(f16[128,896]{1,0:T(8,128)(2,1)S(1)} %get-tuple-element.16), channel_id=1, source_target_pairs={{0,16},{16,32},{32,48},{48,64},{64,80},{80,96},{96,112},{112,0},{1... | collective-permute-start | bytes 688136 | tf_op jit(solution)/shard_map/ppermute | solution.py:18
  84.4 27.5 %collective-permute-start.28 = (f16[128,896]{1,0:T(8,128)(2,1)}, f16[128,896]{1,0:T(8,128)(2,1)}, u32[]{:S(2)}, u32[]{:S(2)}) collective-permute-start(f16[128,896]{1,0:T(8,128)(2,1)} %get-tuple-element.17), channel_id=1, source_target_pairs={{0,112},{16,0},{32,16},{48,32},{64,48},{80,64},{96,80},{112,96},{1... | collective-permute-start | bytes 688136 | tf_op jit(solution)/shard_map/ppermute | solution.py:18
  95.3 20.7 %collective-permute-start.25 = (f16[256,896]{1,0:T(8,128)(2,1)}, f16[256,896]{1,0:T(8,128)(2,1)}, u32[]{:S(2)}, u32[]{:S(2)}) collective-permute-start(f16[256,896]{1,0:T(8,128)(2,1)} %pad_maximum_fusion.6), channel_id=1, source_target_pairs={{0,16},{16,32},{32,48},{48,64},{64,80},{80,96},{96,112},{112,0},{1... | collective-permute-start | bytes 1376264 | tf_op jit(solution)/shard_map/ppermute | solution.py:18
  95.3 0.9 copy-start.9
  107.3 5.7 %copy-start.8 = (f16[128,896]{1,0:T(8,128)(2,1)S(1)}, f16[128,896]{1,0:T(8,128)(2,1)}, u32[]{:S(2)}) copy-start(f16[128,896]{1,0:T(8,128)(2,1)} %fusion.19) | copy-start | bytes 688132
  107.3 21.8 %slice-start.2 = ((s8[5505024]{0:T(1024)(128)(4,1)}), s8[4194304]{0:T(1024)(128)(4,1)S(1)}, s32[]{:S(2)}) async-start(s8[5505024]{0:T(1024)(128)(4,1)} %bitcast.125), calls=%async_computation.2 | async-start | bytes 8388608
  109.1 14.2 %collective-permute-start.2 = (f32[512,256]{1,0:T(8,128)S(1)}, f32[512,256]{1,0:T(8,128)S(1)}, u32[]{:S(2)}, u32[]{:S(2)}) collective-permute-start(f32[512,256]{1,0:T(8,128)S(1)} %get-tuple-element.10), channel_id=1, source_target_pairs={{0,2},{2,4},{4,6},{6,0},{1,3},{3,5},{5,7},{7,1},{8,10},{10,12},{12... | collective-permute-start | bytes 1572872 | tf_op jit(solution)/shard_map/ppermute | solution.py:18
  109.2 14.1 %collective-permute-start.4 = (f32[512,256]{1,0:T(8,128)S(1)}, f32[512,256]{1,0:T(8,128)S(1)}, u32[]{:S(2)}, u32[]{:S(2)}) collective-permute-start(f32[512,256]{1,0:T(8,128)S(1)} %get-tuple-element.11), channel_id=1, source_target_pairs={{0,6},{2,0},{4,2},{6,4},{1,7},{3,1},{5,3},{7,5},{8,14},{10,8},{12,... | collective-permute-start | bytes 1572872 | tf_op jit(solution)/shard_map/ppermute | solution.py:18
  111.9 11.4 %copy-start.5 = (f32[8,512,256]{2,1,0:T(8,128)S(1)}, f32[8,512,256]{2,1,0:T(8,128)}, u32[]{:S(2)}) copy-start(f32[8,512,256]{2,1,0:T(8,128)} %out_parts.1) | copy-start | bytes 12582916
  113.2 15.9 %slice-start.3 = ((s8[5505024]{0:T(1024)(128)(4,1)}), s8[1310720]{0:T(1024)(128)(4,1)S(1)}, s32[]{:S(2)}) async-start(s8[5505024]{0:T(1024)(128)(4,1)} %bitcast.125), calls=%async_computation.3 | async-start | bytes 2621440
  113.2 13.3 %collective-permute-start.29 = (f16[256,896]{1,0:T(8,128)(2,1)S(1)}, f16[256,896]{1,0:T(8,128)(2,1)S(1)}, u32[]{:S(2)}, u32[]{:S(2)}) collective-permute-start(f16[256,896]{1,0:T(8,128)(2,1)S(1)} %pad_maximum_fusion.7), channel_id=1, source_target_pairs={{0,112},{16,0},{32,16},{48,32},{64,48},{80,64},{96,80},{112,96},{1... | collective-permute-start | bytes 1376264 | tf_op jit(solution)/shard_map/ppermute | solution.py:18
  117.4 11.7 %collective-permute-start.26 = (f16[256,896]{1,0:T(8,128)(2,1)S(1)}, f16[256,896]{1,0:T(8,128)(2,1)S(1)}, u32[]{:S(2)}, u32[]{:S(2)}) collective-permute-start(f16[256,896]{1,0:T(8,128)(2,1)S(1)} %fusion.2), channel_id=1, source_target_pairs={{0,16},{16,32},{32,48},{48,64},{64,80},{80,96},{96,112},{112,0},{1... | collective-permute-start | bytes 1376264 | tf_op jit(solution)/shard_map/ppermute | solution.py:18
  123.6 23.3 %collective-permute-start.5 = (f32[2,512,256]{2,1,0:T(8,128)S(1)}, f32[2,512,256]{2,1,0:T(8,128)S(1)}, u32[]{:S(2)}, u32[]{:S(2)}) collective-permute-start(f32[2,512,256]{2,1,0:T(8,128)S(1)} %pad_maximum_fusion.2), channel_id=1, source_target_pairs={{0,6},{2,0},{4,2},{6,4},{1,7},{3,1},{5,3},{7,5},{8,14},{10,8},{12,... | collective-permute-start | bytes 3145736 | tf_op jit(solution)/shard_map/ppermute | solution.py:18
  126.1 3.5 %copy-start.4 = (bf16[1,2,512,256]{3,2,1,0:T(8,128)(2,1)S(1)}, bf16[1,2,512,256]{3,2,1,0:T(8,128)(2,1)}, u32[]{:S(2)}) copy-start(bf16[1,2,512,256]{3,2,1,0:T(8,128)(2,1)} %copy-done.3) | copy-start | bytes 1572868
  126.1 24.2 %collective-permute-start.3 = (f32[2,512,256]{2,1,0:T(8,128)S(1)}, f32[2,512,256]{2,1,0:T(8,128)S(1)}, u32[]{:S(2)}, u32[]{:S(2)}) collective-permute-start(f32[2,512,256]{2,1,0:T(8,128)S(1)} %pad_maximum_fusion.1), channel_id=1, source_target_pairs={{0,2},{2,4},{4,6},{6,0},{1,3},{3,5},{5,7},{7,1},{8,10},{10,12},{12... | collective-permute-start | bytes 3145736 | tf_op jit(solution)/shard_map/ppermute | solution.py:18
  129.1 21.5 %slice-start = ((s8[7340032]{0:T(1024)(128)(4,1)}), s8[3145728]{0:T(1024)(128)(4,1)S(1)}, s32[]{:S(2)}) async-start(s8[7340032]{0:T(1024)(128)(4,1)} %bitcast.123), calls=%async_computation | async-start | bytes 6291456
  129.5 9.6 %collective-permute-start.30 = (f16[256,896]{1,0:T(8,128)(2,1)S(1)}, f16[256,896]{1,0:T(8,128)(2,1)S(1)}, u32[]{:S(2)}, u32[]{:S(2)}) collective-permute-start(f16[256,896]{1,0:T(8,128)(2,1)S(1)} %get-tuple-element.4), channel_id=1, source_target_pairs={{0,112},{16,0},{32,16},{48,32},{64,48},{80,64},{96,80},{112,96},{1... | collective-permute-start | bytes 1376264 | tf_op jit(solution)/shard_map/ppermute | solution.py:18
  129.6 20.9 %slice-start.1 = ((s8[7340032]{0:T(1024)(128)(4,1)}), s8[4194304]{0:T(1024)(128)(4,1)S(1)}, s32[]{:S(2)}) async-start(s8[7340032]{0:T(1024)(128)(4,1)} %bitcast.123), calls=%async_computation.1 | async-start | bytes 8388608
  131.2 19.4 %copy-start.2 = (bf16[4,512,256]{2,1,0:T(8,128)(2,1)S(1)}, bf16[4,512,256]{2,1,0:T(8,128)(2,1)}, u32[]{:S(2)}) copy-start(bf16[4,512,256]{2,1,0:T(8,128)(2,1)} %pad_maximum_fusion.3.refs_0_) | copy-start | bytes 3145732
  131.2 27.6 %collective-permute-start.27 = (f16[256,896]{1,0:T(8,128)(2,1)S(1)}, f16[256,896]{1,0:T(8,128)(2,1)S(1)}, u32[]{:S(2)}, u32[]{:S(2)}) collective-permute-start(f16[256,896]{1,0:T(8,128)(2,1)S(1)} %get-tuple-element.3), channel_id=1, source_target_pairs={{0,16},{16,32},{32,48},{48,64},{64,80},{80,96},{96,112},{112,0},{1... | collective-permute-start | bytes 1376264 | tf_op jit(solution)/shard_map/ppermute | solution.py:18
  139.3 19.5 %collective-permute-start.31 = (f16[256,896]{1,0:T(8,128)(2,1)S(1)}, f16[256,896]{1,0:T(8,128)(2,1)S(1)}, u32[]{:S(2)}, u32[]{:S(2)}) collective-permute-start(f16[256,896]{1,0:T(8,128)(2,1)S(1)} %fusion.1), channel_id=1, source_target_pairs={{0,112},{16,0},{32,16},{48,32},{64,48},{80,64},{96,80},{112,96},{1... | collective-permute-start | bytes 1376264 | tf_op jit(solution)/shard_map/ppermute | solution.py:18
  150.5 10.7 %collective-permute-start.6 = (f32[512,256]{1,0:T(8,128)S(1)}, f32[512,256]{1,0:T(8,128)S(1)}, u32[]{:S(2)}, u32[]{:S(2)}) collective-permute-start(f32[512,256]{1,0:T(8,128)S(1)} %fusion.6), channel_id=1, source_target_pairs={{0,8},{8,0},{1,9},{9,1},{2,10},{10,2},{3,11},{11,3},{4,12},{12,4},... | collective-permute-start | bytes 1572872 | tf_op jit(solution)/shard_map/ppermute | solution.py:18

commit v2 on v1

v2 whole, which is shorter than its diff:
```python
import jax
import jax.numpy as jnp
from jax import lax
from jax.experimental import pallas as pl
from jax.experimental.pallas import tpu as pltpu
from jax.sharding import Mesh
from jax.sharding import PartitionSpec as P


YH, Z, YL, X, C = "yh", "z", "yl", "x", "c"
F32, F16, BF16 = jnp.float32, jnp.float16, jnp.bfloat16
VMEM = pltpu.VMEM


def turned(axis, by):
    def move(array):
        n = lax.axis_size(axis)
        return lax.ppermute(array, axis, [(i, (i + by) % n) for i in range(n)])

    return move


def outward(axis):
    def move(array):
        n = lax.axis_size(axis)
        pairs = [((i, 0), ((i + 1) % n, 0)) for i in range(n)]
        pairs += [((i, 1), ((i - 1) % n, 1)) for i in range(n)]
        flat = [(a * 2 + p, b * 2 + q) for (a, p), (b, q) in pairs]
        return lax.ppermute(array, (axis, C), flat)

    return move


x_out, z_out = outward(X), outward(Z)
other_core, other_yl, other_yh = turned(C, 1), turned(YL, 1), turned(YH, 1)


def pick(array, index):
    return lax.dynamic_index_in_dim(array, index, 0, keepdims=False)


def dot(a, b, da, db):
    return lax.dot_general(a, b, (((da,), (db,)), ((), ())), preferred_element_type=F32)


def table(values):
    return jnp.array(values, jnp.int32)


def cost(flops, bytes_accessed):
    return pl.CostEstimate(flops=flops, bytes_accessed=bytes_accessed, transcendentals=0)


def out_parts(hidden, hidden_c, weight, weight_c, order):
    t, u = hidden.shape
    n, r = order.shape[0], 256

    def kernel(order_ref, h_ref, hc_ref, w_ref, wc_ref, *rest):
        outs, (h_t, rows, sums, sems, out_sems) = rest[:3], rest[3:]

        def fetch(i):
            at = pl.ds(pl.multiple_of(order_ref[i] * r, r), r)
            return [
                pltpu.make_async_copy(ref.at[at], rows.at[i, p], sems.at[i, p])
                for p, ref in enumerate((w_ref, wc_ref))
            ]

        for i in range(n):
            for copy in fetch(i):
                copy.start()
        h_t[0], h_t[1] = h_ref[...].T, hc_ref[...].T
        places = [out.at[i] for out in outs for i in range(out.shape[0])]
        for i in range(n):
            for copy in fetch(i):
                copy.wait()
            sums[i] = dot(rows[i, 0], h_t[0], 1, 0) + dot(rows[i, 1], h_t[1], 1, 0)
            pltpu.make_async_copy(sums.at[i], places[i], out_sems.at[i]).start()
        for i in range(n):
            pltpu.make_async_copy(sums.at[i], places[i], out_sems.at[i]).wait()

    vmem, hbm = pl.BlockSpec(memory_space=VMEM), pl.BlockSpec(memory_space=pltpu.HBM)
    return pl.pallas_call(
        kernel,
        in_specs=[pl.BlockSpec(memory_space=pltpu.SMEM), vmem, vmem, hbm, hbm],
        out_specs=[hbm] * 3,
        out_shape=[jax.ShapeDtypeStruct((k, r, t), F32) for k in (2, 4, 2)],
        scratch_shapes=[
            VMEM((2, u, t), BF16),
            VMEM((n, 2, r, u), BF16),
            VMEM((n, r, t), F32),
            pltpu.SemaphoreType.DMA((n, 2)),
            pltpu.SemaphoreType.DMA((n,)),
        ],
        compiler_params=pltpu.CompilerParams(vmem_limit_bytes=52 << 20),
        cost_estimate=cost(4 * n * t * r * u, 4 * n * t * r),
        name="out_parts",
    )(order, hidden, hidden_c, weight, weight_c)


def grad_parts(blocks, places, hiddens, first, count, own):
    _, t, r = blocks[0].shape
    u = hiddens[0].shape[1]
    m = len(blocks)
    half = first == 0
    rows = r // 2 if half else r

    def kernel(table_ref, *refs):
        blks, (h0, h1, k0, k1), outs = refs[:m], refs[m : m + 4], refs[m + 4 : -2]
        chosen, flipped = refs[-2:]

        def choose(j):
            for i, blk in enumerate(blks):

                @pl.when(table_ref[j] == i)
                def _():
                    if half:
                        for c in range(2):

                            @pl.when(table_ref[7] == c)
                            def _():
                                chosen[...] = blk[:, :, c * rows : (c + 1) * rows]
                    else:
                        chosen[...] = blk[...]

            for i in range(2):
                flipped[i] = chosen[i].T

        for j in range(count):
            choose(first + j)
            outs[0][j, 0] = dot(flipped[0], h0[...], 1, 0) + dot(flipped[1], h1[...], 1, 0)
            outs[0][j, 1] = dot(flipped[0], k0[...], 1, 0) + dot(flipped[1], k1[...], 1, 0)
        if own:
            choose(first + count)
            outs[1][...] = dot(flipped[0], h0[...], 1, 0) + dot(flipped[1], h1[...], 1, 0)

    shapes = [jax.ShapeDtypeStruct((count, 2, rows, u), F32)]
    if own:
        shapes.append(jax.ShapeDtypeStruct((r, u), F32))
    vmem = pl.BlockSpec(memory_space=VMEM)
    work = 4 * count + 2 * own
    return pl.pallas_call(
        kernel,
        in_specs=[pl.BlockSpec(memory_space=pltpu.SMEM)] + [vmem] * (m + 4),
        out_specs=[vmem] * len(shapes),
        out_shape=shapes,
        scratch_shapes=[VMEM((2, t, rows), BF16), VMEM((2, rows, t), BF16)],
        compiler_params=pltpu.CompilerParams(vmem_limit_bytes=18 << 20),
        cost_estimate=cost(2 * work * t * rows * u, 4 * work * rows * u),
        name="grad_parts",
    )(places, *blocks, *hiddens)


def hidden_gradient(blocks, weight, order):
    t, r = blocks[0].shape[1:]
    u = weight.shape[1]
    m = len(blocks)
    n = sum(b.shape[0] for b in blocks) // 4
    assert m == 4

    def kernel(order_ref, *refs):
        cots, ws, o_ref, acc_ref = refs[:m], refs[m : 2 * m], refs[2 * m], refs[2 * m + 1]
        i = pl.program_id(0)
        total = dot(cots[0][0], ws[0][...], 1, 0)
        for a in range(1, m):
            total += dot(cots[a][0], ws[a][...], 1, 0)

        @pl.when(i == 0)
        def _():
            acc_ref[...] = total

        @pl.when(i > 0)
        def _():
            acc_ref[...] += total

        @pl.when(i == n - 1)
        def _():
            o_ref[...] = acc_ref[...].astype(BF16)

    part = pl.BlockSpec((1, t, r), lambda i, o: (i, 0, 0))
    rows = [pl.BlockSpec((r, u), lambda i, o, a=a: (o[a * n + i], 0)) for a in range(m)]
    return pl.pallas_call(
        kernel,
        grid_spec=pltpu.PrefetchScalarGridSpec(
            num_scalar_prefetch=1,
            grid=(n,),
            in_specs=[part] * m + rows,
            out_specs=pl.BlockSpec((t, u), lambda i, o: (0, 0)),
            scratch_shapes=[VMEM((t, u), F32)],
        ),
        out_shape=jax.ShapeDtypeStruct((t, u), BF16),
        compiler_params=pltpu.CompilerParams(vmem_limit_bytes=14 << 20),
        cost_estimate=cost(2 * m * n * t * r * u, 2 * m * n * (t * r + r * u)),
        name="hidden_gradient",
    )(order, *blocks, *([weight] * m))


def layer(hidden, weight, cotangent):
    tokens, _ = hidden.shape
    rows = cotangent.shape[1]
    scale = float(tokens * 16) ** -0.5
    yh, z, yl, x, c = (lax.axis_index(a) for a in (YH, Z, YL, X, C))

    far = lax.ppermute(cotangent, (YH, YL), [(2, 0), (1, 3)])
    near = lax.ppermute(cotangent, (YH, YL), [(2, 1), (1, 2)])
    sib = other_yl(cotangent)
    hidden2 = other_yh(hidden)
    hidden_c = other_core(hidden)
    weight_c = other_core(weight)
    hidden2_c = other_core(hidden2)
    own = yl == yh
    crit = jnp.stack([jnp.where(own, cotangent, sib), far + near])
    rest = jnp.where(own, sib, cotangent)

    a1 = x_out(crit)
    crit_c = other_core(crit)
    a2 = x_out(crit_c)
    a3 = x_out(a1)
    b1 = other_core(a1)
    b2 = other_core(a2)
    b3 = other_core(a3)
    rest_c = other_core(rest)
    r1 = x_out(jnp.stack([rest, rest_c]))
    r2 = x_out(r1[0])
    r1_c = other_core(r1)
    r2_c = other_core(r2)

    ahead = 1 - 2 * c
    at_x = x + table([2, 2, 0, 0, 0, 0, 0, 0]) + ahead * table([0, 0, 1, 1, 1, 1, 0, 0])
    at_y = c * table([1, 1, 1, 1, 0, 0, 0, 0]) + (1 - c) * table([0, 0, 0, 0, 1, 1, 0, 0])
    at_y += yl * table([0, 0, 0, 0, 0, 0, 1, 0]) + (1 - yl) * table([0, 0, 0, 0, 0, 0, 0, 1])
    at_c = table([0, 1, 0, 1, 0, 1, 0, 0]) + c * table([0, 0, 0, 0, 0, 0, 1, 1])
    order = at_y * 8 + at_x % 4 * 2 + at_c
    first, following, last = out_parts(hidden, hidden_c, weight, weight_c, order)
    came = x_out(first)
    came = x_out(jnp.concatenate([following[:2] + came, following[2:]], 0))
    came = came.reshape(2, 2, rows, tokens)
    for_other = lax.dynamic_index_in_dim(came, 1 - c, 1, keepdims=False)
    from_other = other_core(for_other)
    for_own = lax.dynamic_index_in_dim(came, c, 1, keepdims=False)
    keep = last[0] + (pick(for_own, (yl + c) % 2) + pick(from_other, (yl + 1 + c) % 2))
    give = last[1] + (pick(for_own, (yl + 1 + c) % 2) + pick(from_other, (yl + c) % 2))
    given = other_yl(give)
    output = (keep + given).T.astype(BF16)

    blocks = [crit, crit_c, a1, a2, b2, b1, a3, b3]

    d = (z + ahead * table([4, 3, 2, 1, 0, 0, 0, 0])) % 8
    k = (x - d // 2) % 4
    at = jnp.where(k == 0, 0, jnp.where(k == 2, 6, jnp.where((k == 1) == (c == 0), 2, 4)))
    places = (at + (d + c) % 2) * table([1, 1, 1, 1, 1, 0, 0, 0]) + c * table([0, 0, 0, 0, 0, 1, 1, 1])
    hiddens = [hidden, hidden2, hidden_c, hidden2_c]
    (g0,) = grad_parts(blocks, places, hiddens, 0, 1, False)
    g, g_own = grad_parts(blocks, places, hiddens, 1, 3, True)
    came = z_out((g0[0] * 0.25).astype(F16))
    came = came.astype(F32)
    low = jnp.concatenate([jnp.where(c == 0, came, 0.0), jnp.where(c == 0, 0.0, came)], 1)
    came = z_out((g[0] * 0.25 + low).astype(F16))
    came = z_out((g[1] * 0.25 + came.astype(F32)).astype(F16))
    came = z_out((g[2] * 0.25 + came.astype(F32)).astype(F16))
    came_c = other_core(came)[1]
    weight_grad = g_own * scale + (came[0].astype(F32) + came_c.astype(F32)) * (scale * 4.0)

    mine = jnp.stack([crit[0], a1[0], b2[0], a3[0]])
    theirs = jnp.stack([crit_c[0], a2[0], b1[0], b3[0]])
    rest_m = jnp.stack([rest, r1[0], r1_c[1], r2])
    rest_t = jnp.stack([rest_c, r1[1], r1_c[0], r2_c])
    y = yh * table([1] * 8 + [0] * 8) + (1 - yh) * table([0] * 8 + [1] * 8)
    cc = c * table([1, 1, 1, 1, 0, 0, 0, 0] * 2) + (1 - c) * table([0, 0, 0, 0, 1, 1, 1, 1] * 2)
    order = y * 8 + (x + table([0, 0, 0, 2] * 4) + ahead * table([0, -1, 1, 0] * 4)) % 4 * 2 + cc
    hidden_grad = hidden_gradient([mine, theirs, rest_m, rest_t], weight, order)
    return output, hidden_grad, weight_grad


def solution(mesh):
    finer = Mesh(mesh.devices.reshape(2, 8, 2, 4, 2), (YH, Z, YL, X, C))
    gx, gy = (YH, Z), (YL, X, C)
    return jax.shard_map(
        layer,
        mesh=finer,
        in_specs=(P(gx, gy), P(None, gy), P(gx, gy)),
        out_specs=(P(gx, gy), P(gx, gy), P(gx, gy)),
        check_vma=False,
    )
```

time: 163 us -> 166 us (1.018)
  waiting for transfers between devices: 67.4 us -> 48.3 us
  starting transfers between devices: 45.6 us -> 62.1 us
  local copies, waits for them, and re-layouts: 8.05 us -> 13.9 us
    ppermute x30 -> x15, waiting for transfers between devices: 62.5 us -> 12.2 us  [move(): return lax.ppermute(array, axis, [(i, (i + by) % n) for i in range(n)])]
    ppermute x0 -> x11, waiting for transfers between devices: none -> 31.4 us  [move(): return lax.ppermute(array, (axis, C), flat)]
    ppermute x0 -> x11, starting transfers between devices: none -> 25.8 us  [move(): return lax.ppermute(array, (axis, C), flat)]
    ppermute x30 -> x15, starting transfers between devices: 43.6 us -> 34.3 us  [move(): return lax.ppermute(array, axis, [(i, (i + by) % n) for i in range(n)])]
    slice x2 -> x10, local copies, waits for them, and re-layouts: 0.02 us -> 9.18 us  [the longest x5 4.1 us: layer(): theirs = jnp.stack([crit_c[0], a2[0], b1[0], b3[0]])]
    add x2 -> x6, other arithmetic: 0.17 us -> 3.93 us  [the longest x1 2.14 us: layer(): g_own * scale + (came[0].astype(F32) + came_c.astype(F32)) * (scale * 4.0)]
    convert_element_type x4 -> x5, other arithmetic: 2.95 us -> 5.81 us  [the longest x1 2.75 us: layer(): came = z_out((g[2] * 0.25 + came.astype(F32)).astype(F16))]
    another operation x11 -> x7, other arithmetic: 4.01 us -> 1.61 us  [the longest x1 1.08 us: layer(): rest_m = jnp.stack([rest, r1[0], r1_c[1], r2])]
  transfers between devices with their start and end apart: 32 -> 28, of which waited for: 16 -> 13; matrix products, arithmetic and copies ran while one was open for 11% -> 13% of each run, Pallas kernels for 16% -> 15%
where the time goes in v2:
time: 166 us
  starting transfers between devices  62.1 us (37%)
  waiting for transfers between devices  48.3 us (29%)
  Pallas kernels  25.6 us (15%)
  other arithmetic  14.7 us (9%)
  local copies, waits for them, and re-layouts  13.9 us (8%)
    ppermute x15, starting transfers between devices, move(): return lax.ppermute(array, axis, [(i, (i + by) % n) for i in range(n)])  34.3 us
    ppermute x11, waiting for transfers between devices, move(): return lax.ppermute(array, (axis, C), flat)  31.4 us
    ppermute x11, starting transfers between devices, move(): return lax.ppermute(array, (axis, C), flat)  25.8 us
    ppermute x15, waiting for transfers between devices, move(): return lax.ppermute(array, axis, [(i, (i + by) % n) for i in range(n)])  12.2 us
    pallas_call x2, Pallas kernels, grad_parts(): pl.pallas_call(kernel, in_specs=[pl.BlockSpec(memory_space=pltpu.SMEM)] +...  9.95 us
    pallas_call x1, Pallas kernels, out_parts(): pl.pallas_call(kernel, in_specs=[pl.BlockSpec(memory_space=pltpu.SMEM), v...  8.38 us
    pallas_call x1, Pallas kernels, hidden_gradient(): pl.pallas_call(kernel, grid_spec=pltpu.PrefetchScalarGridSpec(num_scalar_...  7.26 us
    ppermute x1, waiting for transfers between devices, layer(): far = lax.ppermute(cotangent, (YH, YL), [(2, 0), (1, 3)])  4.67 us
  transfers between devices with their start and end apart: 28, of which 13 were waited for; matrix products, arithmetic and copies ran while one was open for 13% of the time, Pallas kernels for 15%

profile of v2, /device:TPU:1, one launch (start us, length us, event | category | flops | bytes accessed | tf_op | source)
XLA Modules:
  0.0 165.9 jit_solution(4402798122899431587)
XLA Ops:
  0.8 3.3 %collective-permute-start.1 = (bf16[4096,896]{1,0:T(8,128)(2,1)}, bf16[4096,896]{1,0:T(8,128)(2,1)}, u32[]{:S(2)}, u32[]{:S(2)}) collective-permute-start(bf16[4096,896]{1,0:T(8,128)(2,1)} %refs_7_.1), channel_id=1, source_target_pairs={{0,1},{1,0},{2,3},{3,2},{4,5},{5,4},{6,7},{7,6},{8,9},{9,8},{10,11... | collective-permute-start | bytes 22020104 | tf_op jit(solution)/shard_map/ppermute | solution.py:18
  4.1 1.3 collective-permute-start.7
  5.4 0.7 collective-permute-start.8
  6.0 5.8 %collective-permute-start.21 = (bf16[512,896]{1,0:T(8,128)(2,1)}, bf16[512,896]{1,0:T(8,128)(2,1)}, u32[]{:S(2)}, u32[]{:S(2)}) collective-permute-start(bf16[512,896]{1,0:T(8,128)(2,1)} %refs_8_.3), channel_id=1, source_target_pairs={{0,128},{128,0},{1,129},{129,1},{2,130},{130,2},{3,131},{131,3},{4... | collective-permute-start | bytes 2752520 | tf_op jit(solution)/shard_map/ppermute | solution.py:18
  11.8 0.2 collective-permute-done.6
  12.0 1.7 %broadcast_select_fusion = (bf16[512,256]{1,0:T(8,128)(2,1)}, bf16[1,512,256]{2,1,0:T(8,128)(2,1)S(1)}) fusion(bf16[512,256]{1,0:T(8,128)(2,1)S(1)} %collective-permute-done.6, bf16[512,256]{1,0:T(8,128)(2,1)} %param.22, pred[]{:T(512)S(6)} %eq.35), kind=kLoop, calls=%fused_computation.29 | loop fusion | flops 262144 | bytes 1048577 | tf_op jit(solution)/shard_map/jit(_where)/select_n | solution.py:212
  13.7 4.7 %collective-permute-done.7 = bf16[512,256]{1,0:T(8,128)(2,1)S(1)} collective-permute-done((bf16[512,256]{1,0:T(8,128)(2,1)}, bf16[512,256]{1,0:T(8,128)(2,1)S(1)}, u32[]{:S(2)}, u32[]{:S(2)}) %collective-permute-start.7) | collective-permute-done | bytes 262176 | tf_op jit(solution)/shard_map/ppermute | solution.py:203
  18.5 1.6 collective-permute-start.10
  20.1 2.5 %collective-permute-start.9 = (bf16[2,512,256]{2,1,0:T(8,128)(2,1)S(1)}, bf16[2,512,256]{2,1,0:T(8,128)(2,1)}, u32[]{:S(2)}, u32[]{:S(2)}) collective-permute-start(bf16[2,512,256]{2,1,0:T(8,128)(2,1)S(1)} %pad_maximum_fusion.5.refs_0_), channel_id=1, source_target_pairs={{0,2},{2,4},{4,6},{6,0},{1,7},{3,1},{5,3},{7,5},{8,10},{10,12},{12... | collective-permute-start | bytes 1572872 | tf_op jit(solution)/shard_map/ppermute | solution.py:29
  22.6 1.5 collective-permute-start.11
  24.1 0.8 copy-done.3
  24.9 3.8 %collective-permute-done.9.refs_2_ = bf16[2,512,256]{2,1,0:T(8,128)(2,1)} collective-permute-done((bf16[2,512,256]{2,1,0:T(8,128)(2,1)S(1)}, bf16[2,512,256]{2,1,0:T(8,128)(2,1)}, u32[]{:S(2)}, u32[]{:S(2)}) %collective-permute-start.9) | collective-permute-done | bytes 524320 | tf_op jit(solution)/shard_map/ppermute | solution.py:29
  28.7 3.5 %collective-permute-start.13 = (bf16[2,512,256]{2,1,0:T(8,128)(2,1)}, bf16[2,512,256]{2,1,0:T(8,128)(2,1)}, u32[]{:S(2)}, u32[]{:S(2)}) collective-permute-start(bf16[2,512,256]{2,1,0:T(8,128)(2,1)} %collective-permute-done.9.refs_2_), channel_id=1, source_target_pairs={{0,2},{2,4},{4,6},{6,0},{1,7},{3,1},{5,3},{7,5},{8,10},{10,12},{12... | collective-permute-start | bytes 1572872 | tf_op jit(solution)/shard_map/ppermute | solution.py:29
  32.2 5.9 %collective-permute-done.21.refs_9_ = bf16[512,896]{1,0:T(8,128)(2,1)} collective-permute-done((bf16[512,896]{1,0:T(8,128)(2,1)}, bf16[512,896]{1,0:T(8,128)(2,1)}, u32[]{:S(2)}, u32[]{:S(2)}) %collective-permute-start.21) | collective-permute-done | bytes 917536 | tf_op jit(solution)/shard_map/ppermute | solution.py:18
  38.2 1.0 collective-permute-start.22
  39.1 0.5 collective-permute-start.12
  39.6 0.4 collective-permute-done.13.refs_6_
  40.1 1.9 %collective-permute-start.15 = (bf16[2,512,256]{2,1,0:T(8,128)(2,1)}, bf16[2,512,256]{2,1,0:T(8,128)(2,1)S(1)}, u32[]{:S(2)}, u32[]{:S(2)}) collective-permute-start(bf16[2,512,256]{2,1,0:T(8,128)(2,1)} %collective-permute-done.13.refs_6_), channel_id=1, source_target_pairs={{0,1},{1,0},{2,3},{3,2},{4,5},{5,4},{6,7},{7,6},{8,9},{9,8},{10,11... | collective-permute-start | bytes 1572872 | tf_op jit(solution)/shard_map/ppermute | solution.py:18
  42.1 0.2 collective-permute-done.14.refs_5_
  42.3 0.6 collective-permute-done.12.refs_4_
  42.9 0.7 collective-permute-done.15.refs_7_
  43.7 1.2 copy-done.4
  44.9 3.0 %grad_parts.3 = f32[1,2,128,896]{3,2,1,0:T(8,128)S(1)} custom-call(s32[8]{0:T(128)S(1)} %multiply_add_fusion.table_ref, bf16[2,512,256]{2,1,0:T(8,128)(2,1)S(1)} %pad_maximum_fusion.5.refs_0_, bf16[2,512,256]{2,1,0:T(8,128)(2,1)S(1)} %copy-done.4, bf16[2,512,256]{2,1,0:T(8,128)(2,1)} %collective-permute-done.9.refs_2_, ...), custom_call_target="tpu_custom_call" | custom-call | flops 469762048 | bytes 1835008 | tf_op jit(solution)/shard_map/grad_parts/pallas_call | solution.py:141
  48.0 5.8 %collective-permute-start.23 = (f16[2,128,896]{2,1,0:T(8,128)(2,1)S(1)}, f16[2,128,896]{2,1,0:T(8,128)(2,1)S(1)}, u32[]{:S(2)}, u32[]{:S(2)}) collective-permute-start(f16[2,128,896]{2,1,0:T(8,128)(2,1)S(1)} %fusion.7), channel_id=1, source_target_pairs={{0,16},{16,32},{32,48},{48,64},{64,80},{80,96},{96,112},{112,0},{1... | collective-permute-start | bytes 1376264 | tf_op jit(solution)/shard_map/ppermute | solution.py:29
  53.8 8.4 %out_parts.1 = (f32[2,256,512]{2,1,0:T(8,128)}, f32[4,256,512]{2,1,0:T(8,128)}, f32[2,256,512]{2,1,0:T(8,128)}) custom-call(s32[8]{0:T(128)S(1)} %fusion.12.order_ref, bf16[512,896]{1,0:T(8,128)(2,1)S(1)} %copy-done.1, bf16[512,896]{1,0:T(8,128)(2,1)S(1)} %collective-permute-done.hc_ref.refs_10_, bf16[4096,896]{1,0:T(8,128)(2,1)} %refs_7_.1, ...), custom_call_target="tpu_custom_call" | custom-call | flops 3758096384 | bytes 4194304 | tf_op jit(solution)/shard_map/out_parts/pallas_call | solution.py:82
  62.2 2.6 %collective-permute-start.2 = (f32[2,256,512]{2,1,0:T(8,128)}, f32[2,256,512]{2,1,0:T(8,128)S(1)}, u32[]{:S(2)}, u32[]{:S(2)}) collective-permute-start(f32[2,256,512]{2,1,0:T(8,128)} %get-tuple-element.10), channel_id=1, source_target_pairs={{0,2},{2,4},{4,6},{6,0},{1,7},{3,1},{5,3},{7,5},{8,10},{10,12},{12... | collective-permute-start | bytes 3145736 | tf_op jit(solution)/shard_map/ppermute | solution.py:29
  64.8 7.0 %grad_parts.2 = (f32[3,2,256,896]{3,2,1,0:T(8,128)S(1)}, f32[256,896]{1,0:T(8,128)S(1)}) custom-call(s32[8]{0:T(128)S(1)} %multiply_add_fusion.table_ref, bf16[2,512,256]{2,1,0:T(8,128)(2,1)S(1)} %pad_maximum_fusion.5.refs_0_, bf16[2,512,256]{2,1,0:T(8,128)(2,1)S(1)} %copy-done.5, bf16[2,512,256]{2,1,0:T(8,128)(2,1)} %collective-permute-done.9.refs_2_, ...), custom_call_target="tpu_custom_call" | custom-call | flops 3288334336 | bytes 12845056 | tf_op jit(solution)/shard_map/grad_parts/pallas_call | solution.py:141
  71.9 0.3 fusion
  72.3 0.4 copy-done.7
  72.7 0.7 collective-permute-start.24
  73.4 3.4 %collective-permute-done.2 = f32[2,256,512]{2,1,0:T(8,128)S(1)} collective-permute-done((f32[2,256,512]{2,1,0:T(8,128)}, f32[2,256,512]{2,1,0:T(8,128)S(1)}, u32[]{:S(2)}, u32[]{:S(2)}) %collective-permute-start.2) | collective-permute-done | bytes 1048608 | tf_op jit(solution)/shard_map/ppermute | solution.py:29
  76.8 0.4 slice_add_fusion
  77.2 1.6 pad_maximum_fusion
  78.8 3.3 %collective-permute-start.3 = (f32[4,256,512]{2,1,0:T(8,128)}, f32[4,256,512]{2,1,0:T(8,128)}, u32[]{:S(2)}, u32[]{:S(2)}) collective-permute-start(f32[4,256,512]{2,1,0:T(8,128)} %pad_maximum_fusion), channel_id=1, source_target_pairs={{0,2},{2,4},{4,6},{6,0},{1,7},{3,1},{5,3},{7,5},{8,10},{10,12},{12... | collective-permute-start | bytes 6291464 | tf_op jit(solution)/shard_map/ppermute | solution.py:29
  82.1 3.3 %collective-permute-done.24 = f16[2,256,896]{2,1,0:T(8,128)(2,1)S(1)} collective-permute-done((f16[2,256,896]{2,1,0:T(8,128)(2,1)S(1)}, f16[2,256,896]{2,1,0:T(8,128)(2,1)S(1)}, u32[]{:S(2)}, u32[]{:S(2)}) %collective-permute-start.24) | collective-permute-done | bytes 917536 | tf_op jit(solution)/shard_map/ppermute | solution.py:29
  85.3 1.3 fusion.1
  86.6 1.9 %collective-permute-start.25 = (f16[2,256,896]{2,1,0:T(8,128)(2,1)}, f16[2,256,896]{2,1,0:T(8,128)(2,1)S(1)}, u32[]{:S(2)}, u32[]{:S(2)}) collective-permute-start(f16[2,256,896]{2,1,0:T(8,128)(2,1)} %fusion.1), channel_id=1, source_target_pairs={{0,16},{16,32},{32,48},{48,64},{64,80},{80,96},{96,112},{112,0},{1... | collective-permute-start | bytes 2752520 | tf_op jit(solution)/shard_map/ppermute | solution.py:29
  88.5 1.5 collective-permute-done.16
  90.1 0.2 collective-permute-start.17
  90.4 20.5 %collective-permute-done.17 = bf16[2,512,256]{2,1,0:T(8,128)(2,1)} collective-permute-done((bf16[2,512,256]{2,1,0:T(8,128)(2,1)S(1)}, bf16[2,512,256]{2,1,0:T(8,128)(2,1)}, u32[]{:S(2)}, u32[]{:S(2)}) %collective-permute-start.17) | collective-permute-done | bytes 524320 | tf_op jit(solution)/shard_map/ppermute | solution.py:29
  110.9 2.8 %fusion.2 = f16[2,256,896]{2,1,0:T(8,128)(2,1)} fusion(f16[2,256,896]{2,1,0:T(8,128)(2,1)S(1)} %collective-permute-done.25, f32[3,2,256,896]{3,2,1,0:T(8,128)} %copy-done), kind=kLoop, calls=%fused_computation.6 | loop fusion | flops 1835008 | bytes 3670016 | tf_op jit(solution)/shard_map/convert_element_type | solution.py:259
  113.7 3.2 %collective-permute-start.26 = (f16[2,256,896]{2,1,0:T(8,128)(2,1)}, f16[2,256,896]{2,1,0:T(8,128)(2,1)}, u32[]{:S(2)}, u32[]{:S(2)}) collective-permute-start(f16[2,256,896]{2,1,0:T(8,128)(2,1)} %fusion.2), channel_id=1, source_target_pairs={{0,16},{16,32},{32,48},{48,64},{64,80},{80,96},{96,112},{112,0},{1... | collective-permute-start | bytes 2752520 | tf_op jit(solution)/shard_map/ppermute | solution.py:29
  116.9 1.9 %fusion.21 = (bf16[1,512,256]{2,1,0:T(8,128)(2,1)S(1)}, bf16[512,256]{1,0:T(8,128)(2,1)}, bf16[1,512,256]{2,1,0:T(8,128)(2,1)}) fusion(bf16[2,512,256]{2,1,0:T(8,128)(2,1)} %collective-permute-done.17), kind=kLoop, calls=%fused_computation.66 | loop fusion | bytes 1310720 | tf_op jit(solution)/shard_map/slice | solution.py:266
  118.8 0.5 collective-permute-start.19
  119.3 1.3 dynamic-slice_bitcast_fusion
  120.9 1.1 slice.81
  122.0 1.2 slice.85
  123.2 1.0 slice.86
  124.2 1.0 slice.83
  125.2 0.5 collective-permute-start.20
  125.8 1.1 fusion.22
  126.8 1.1 pad_maximum_fusion.3.refs_2_
  127.9 1.3 collective-permute-start.27
  129.2 0.1 pad_maximum_fusion.4.refs_3_
  129.4 0.1 pad_maximum_fusion.1.refs_0_
  129.6 1.9 %slice-done.2 = bf16[1,512,256]{2,1,0:T(8,128)(2,1)S(1)} async-done(((bf16[2,512,256]{2,1,0:T(8,128)(2,1)}), bf16[1,512,256]{2,1,0:T(8,128)(2,1)S(1)}, s32[]{:S(2)}) %slice-start.2) | async-done | bytes 262168 | tf_op jit(solution)/shard_map/slice | solution.py:264
  131.5 0.1 pad_maximum_fusion.2.refs_1_
  131.6 1.4 fusion.3
  133.0 18.4 %collective-permute-start.5 = (f32[256,512]{1,0:T(8,128)S(1)}, f32[256,512]{1,0:T(8,128)S(1)}, u32[]{:S(2)}, u32[]{:S(2)}) collective-permute-start(f32[256,512]{1,0:T(8,128)S(1)} %fusion.3), channel_id=1, source_target_pairs={{0,8},{8,0},{1,9},{9,1},{2,10},{10,2},{3,11},{11,3},{4,12},{12,4},... | collective-permute-start | bytes 1572872 | tf_op jit(solution)/shard_map/ppermute | solution.py:18
  151.4 7.3 %hidden_gradient.1 = bf16[512,896]{1,0:T(8,128)(2,1)} custom-call(s32[16]{0:T(128)S(1)} %fusion.15.order_ref, bf16[4,512,256]{2,1,0:T(8,128)(2,1)S(1)} %pad_maximum_fusion.1.refs_0_, bf16[4,512,256]{2,1,0:T(8,128)(2,1)S(1)} %pad_maximum_fusion.2.refs_1_, bf16[4,512,256]{2,1,0:T(8,128)(2,1)S(1)} %pad_maximum_fusion.3.refs_2_, ...), custom_call_target="tpu_custom_call" | custom-call | flops 3758096384 | bytes 11534336 | tf_op jit(solution)/shard_map/hidden_gradient/pallas_call | solution.py:181
  158.6 2.1 %bitcast_add_fusion.2 = f32[256,896]{1,0:T(8,128)} fusion(f32[256,896]{1,0:T(8,128)S(1)} %copy-done.8, f16[2,256,896]{2,1,0:T(8,128)(2,1)S(1)} %collective-permute-done.27, f16[2,256,896]{2,1,0:T(8,128)(2,1)} %collective-permute-done.26), kind=kLoop, calls=%fused_computation.15 | loop fusion | flops 1376256 | bytes 2752512 | tf_op jit(solution)/shard_map/add | solution.py:261
  160.8 2.9 %collective-permute-done.5 = f32[256,512]{1,0:T(8,128)S(1)} collective-permute-done((f32[256,512]{1,0:T(8,128)S(1)}, f32[256,512]{1,0:T(8,128)S(1)}, u32[]{:S(2)}, u32[]{:S(2)}) %collective-permute-start.5) | collective-permute-done | bytes 524320 | tf_op jit(solution)/shard_map/ppermute | solution.py:18
  163.7 1.4 fusion.8
  165.0 0.8 copy.23
  (102 shorter events, 0.8 us)
Async XLA Ops:
  0.6 41.3 %copy-start.17 = (s32[8]{0:T(128)S(1)}, s32[8]{0:T(128)}, u32[]{:S(2)}) copy-start(s32[8]{0:T(128)} %constant.214.clone) | copy-start | bytes 100
  0.6 41.3 %copy-start.18 = (s32[8]{0:T(128)S(1)}, s32[8]{0:T(128)}, u32[]{:S(2)}) copy-start(s32[8]{0:T(128)} %constant.213.clone) | copy-start | bytes 100
  0.7 41.3 %copy-start.19 = (s32[8]{0:T(128)S(1)}, s32[8]{0:T(128)}, u32[]{:S(2)}) copy-start(s32[8]{0:T(128)} %constant.212.clone) | copy-start | bytes 100
  0.7 41.3 %copy-start.26 = (s32[8]{0:T(128)S(1)}, s32[8]{0:T(128)}, u32[]{:S(2)}) copy-start(s32[8]{0:T(128)} %constant.211.clone) | copy-start | bytes 100
  0.7 41.3 %copy-start.27 = (s32[8]{0:T(128)S(1)}, s32[8]{0:T(128)}, u32[]{:S(2)}) copy-start(s32[8]{0:T(128)} %constant.210.clone) | copy-start | bytes 100
  0.7 41.3 %copy-start.28 = (s32[8]{0:T(128)S(1)}, s32[8]{0:T(128)}, u32[]{:S(2)}) copy-start(s32[8]{0:T(128)} %constant.209.clone) | copy-start | bytes 100
  0.7 41.3 %copy-start.29 = (s32[8]{0:T(128)S(1)}, s32[8]{0:T(128)}, u32[]{:S(2)}) copy-start(s32[8]{0:T(128)} %constant.208.clone) | copy-start | bytes 100
  0.7 41.3 %copy-start.30 = (s32[8]{0:T(128)S(1)}, s32[8]{0:T(128)}, u32[]{:S(2)}) copy-start(s32[8]{0:T(128)} %constant.207.clone) | copy-start | bytes 100
  0.7 41.3 %copy-start.31 = (s32[8]{0:T(128)S(1)}, s32[8]{0:T(128)}, u32[]{:S(2)}) copy-start(s32[8]{0:T(128)} %constant.206.clone) | copy-start | bytes 100
  0.7 41.3 %copy-start.32 = (s32[8]{0:T(128)S(1)}, s32[8]{0:T(128)}, u32[]{:S(2)}) copy-start(s32[8]{0:T(128)} %constant.205.clone) | copy-start | bytes 100
  0.8 41.3 %copy-start.33 = (s32[8]{0:T(128)S(1)}, s32[8]{0:T(128)}, u32[]{:S(2)}) copy-start(s32[8]{0:T(128)} %constant.204.clone) | copy-start | bytes 100
  0.8 21.8 %copy-start.1 = (bf16[512,896]{1,0:T(8,128)(2,1)S(1)}, bf16[512,896]{1,0:T(8,128)(2,1)}, u32[]{:S(2)}) copy-start(bf16[512,896]{1,0:T(8,128)(2,1)} %refs_8_.3) | copy-start | bytes 2752516
  0.8 53.0 %collective-permute-start.1 = (bf16[4096,896]{1,0:T(8,128)(2,1)}, bf16[4096,896]{1,0:T(8,128)(2,1)}, u32[]{:S(2)}, u32[]{:S(2)}) collective-permute-start(bf16[4096,896]{1,0:T(8,128)(2,1)} %refs_7_.1), channel_id=1, source_target_pairs={{0,1},{1,0},{2,3},{3,2},{4,5},{5,4},{6,7},{7,6},{8,9},{9,8},{10,11... | collective-permute-start | bytes 22020104 | tf_op jit(solution)/shard_map/ppermute | solution.py:18
  4.1 8.0 %collective-permute-start.6 = (bf16[512,256]{1,0:T(8,128)(2,1)}, bf16[512,256]{1,0:T(8,128)(2,1)S(1)}, u32[]{:S(2)}, u32[]{:S(2)}) collective-permute-start(bf16[512,256]{1,0:T(8,128)(2,1)} %param.22), channel_id=1, source_target_pairs={{0,8},{8,0},{1,9},{9,1},{2,10},{10,2},{3,11},{11,3},{4,12},{12,4},... | collective-permute-start | bytes 786440 | tf_op jit(solution)/shard_map/ppermute | solution.py:18
  4.1 14.3 %collective-permute-start.7 = (bf16[512,256]{1,0:T(8,128)(2,1)}, bf16[512,256]{1,0:T(8,128)(2,1)S(1)}, u32[]{:S(2)}, u32[]{:S(2)}) collective-permute-start(bf16[512,256]{1,0:T(8,128)(2,1)} %param.22), channel_id=1, source_target_pairs={{128,0},{8,136},{129,1},{9,137},{130,2},{10,138},{131,3},{11,139},... | collective-permute-start | bytes 786440 | tf_op jit(solution)/shard_map/ppermute | solution.py:203
  5.4 13.0 %collective-permute-start.8 = (bf16[512,256]{1,0:T(8,128)(2,1)}, bf16[512,256]{1,0:T(8,128)(2,1)S(1)}, u32[]{:S(2)}, u32[]{:S(2)}) collective-permute-start(bf16[512,256]{1,0:T(8,128)(2,1)} %param.22), channel_id=1, source_target_pairs={{128,8},{8,128},{129,9},{9,129},{130,10},{10,130},{131,11},{11,131... | collective-permute-start | bytes 786440 | tf_op jit(solution)/shard_map/ppermute | solution.py:204
  6.0 32.1 %collective-permute-start.21 = (bf16[512,896]{1,0:T(8,128)(2,1)}, bf16[512,896]{1,0:T(8,128)(2,1)}, u32[]{:S(2)}, u32[]{:S(2)}) collective-permute-start(bf16[512,896]{1,0:T(8,128)(2,1)} %refs_8_.3), channel_id=1, source_target_pairs={{0,128},{128,0},{1,129},{129,1},{2,130},{130,2},{3,131},{131,3},{4... | collective-permute-start | bytes 2752520 | tf_op jit(solution)/shard_map/ppermute | solution.py:18
  13.7 6.4 %copy-start.9 = (bf16[1,512,256]{2,1,0:T(8,128)(2,1)}, bf16[1,512,256]{2,1,0:T(8,128)(2,1)S(1)}, u32[]{:S(2)}) copy-start(bf16[1,512,256]{2,1,0:T(8,128)(2,1)S(1)} %get-tuple-element.24) | copy-start | bytes 786436
  18.5 4.1 %collective-permute-start.10 = (bf16[2,512,256]{2,1,0:T(8,128)(2,1)S(1)}, bf16[2,512,256]{2,1,0:T(8,128)(2,1)S(1)}, u32[]{:S(2)}, u32[]{:S(2)}) collective-permute-start(bf16[2,512,256]{2,1,0:T(8,128)(2,1)S(1)} %pad_maximum_fusion.5.refs_0_), channel_id=1, source_target_pairs={{0,1},{1,0},{2,3},{3,2},{4,5},{5,4},{6,7},{7,6},{8,9},{9,8},{10,11... | collective-permute-start | bytes 1572872 | tf_op jit(solution)/shard_map/ppermute | solution.py:18
  20.1 8.6 %collective-permute-start.9 = (bf16[2,512,256]{2,1,0:T(8,128)(2,1)S(1)}, bf16[2,512,256]{2,1,0:T(8,128)(2,1)}, u32[]{:S(2)}, u32[]{:S(2)}) collective-permute-start(bf16[2,512,256]{2,1,0:T(8,128)(2,1)S(1)} %pad_maximum_fusion.5.refs_0_), channel_id=1, source_target_pairs={{0,2},{2,4},{4,6},{6,0},{1,7},{3,1},{5,3},{7,5},{8,10},{10,12},{12... | collective-permute-start | bytes 1572872 | tf_op jit(solution)/shard_map/ppermute | solution.py:29
  22.6 16.5 %collective-permute-start = (bf16[512,896]{1,0:T(8,128)(2,1)S(1)}, bf16[512,896]{1,0:T(8,128)(2,1)S(1)}, u32[]{:S(2)}, u32[]{:S(2)}) collective-permute-start(bf16[512,896]{1,0:T(8,128)(2,1)S(1)} %copy-done.1), channel_id=1, source_target_pairs={{0,1},{1,0},{2,3},{3,2},{4,5},{5,4},{6,7},{7,6},{8,9},{9,8},{10,11... | collective-permute-start | bytes 2752520 | tf_op jit(solution)/shard_map/ppermute | solution.py:18
  22.6 16.5 %collective-permute-start.11 = (bf16[2,512,256]{2,1,0:T(8,128)(2,1)S(1)}, bf16[2,512,256]{2,1,0:T(8,128)(2,1)}, u32[]{:S(2)}, u32[]{:S(2)}) collective-permute-start(bf16[2,512,256]{2,1,0:T(8,128)(2,1)S(1)} %collective-permute-done.10.refs_1_), channel_id=1, source_target_pairs={{0,2},{2,4},{4,6},{6,0},{1,7},{3,1},{5,3},{7,5},{8,10},{10,12},{12... | collective-permute-start | bytes 1572872 | tf_op jit(solution)/shard_map/ppermute | solution.py:29
  28.7 11.3 %collective-permute-start.13 = (bf16[2,512,256]{2,1,0:T(8,128)(2,1)}, bf16[2,512,256]{2,1,0:T(8,128)(2,1)}, u32[]{:S(2)}, u32[]{:S(2)}) collective-permute-start(bf16[2,512,256]{2,1,0:T(8,128)(2,1)} %collective-permute-done.9.refs_2_), channel_id=1, source_target_pairs={{0,2},{2,4},{4,6},{6,0},{1,7},{3,1},{5,3},{7,5},{8,10},{10,12},{12... | collective-permute-start | bytes 1572872 | tf_op jit(solution)/shard_map/ppermute | solution.py:29
  38.2 5.5 %collective-permute-start.22 = (bf16[512,896]{1,0:T(8,128)(2,1)}, bf16[512,896]{1,0:T(8,128)(2,1)}, u32[]{:S(2)}, u32[]{:S(2)}) collective-permute-start(bf16[512,896]{1,0:T(8,128)(2,1)} %collective-permute-done.21.refs_9_), channel_id=1, source_target_pairs={{0,1},{1,0},{2,3},{3,2},{4,5},{5,4},{6,7},{7,6},{8,9},{9,8},{10,11... | collective-permute-start | bytes 2752520 | tf_op jit(solution)/shard_map/ppermute | solution.py:18
  39.1 3.2 %collective-permute-start.14 = (bf16[2,512,256]{2,1,0:T(8,128)(2,1)}, bf16[2,512,256]{2,1,0:T(8,128)(2,1)}, u32[]{:S(2)}, u32[]{:S(2)}) collective-permute-start(bf16[2,512,256]{2,1,0:T(8,128)(2,1)} %collective-permute-done.9.refs_2_), channel_id=1, source_target_pairs={{0,1},{1,0},{2,3},{3,2},{4,5},{5,4},{6,7},{7,6},{8,9},{9,8},{10,11... | collective-permute-start | bytes 1572872 | tf_op jit(solution)/shard_map/ppermute | solution.py:18
  39.1 3.8 %collective-permute-start.12 = (bf16[2,512,256]{2,1,0:T(8,128)(2,1)}, bf16[2,512,256]{2,1,0:T(8,128)(2,1)S(1)}, u32[]{:S(2)}, u32[]{:S(2)}) collective-permute-start(bf16[2,512,256]{2,1,0:T(8,128)(2,1)} %collective-permute-done.11.refs_3_), channel_id=1, source_target_pairs={{0,1},{1,0},{2,3},{3,2},{4,5},{5,4},{6,7},{7,6},{8,9},{9,8},{10,11... | collective-permute-start | bytes 1572872 | tf_op jit(solution)/shard_map/ppermute | solution.py:18
  40.1 3.6 %collective-permute-start.15 = (bf16[2,512,256]{2,1,0:T(8,128)(2,1)}, bf16[2,512,256]{2,1,0:T(8,128)(2,1)S(1)}, u32[]{:S(2)}, u32[]{:S(2)}) collective-permute-start(bf16[2,512,256]{2,1,0:T(8,128)(2,1)} %collective-permute-done.13.refs_6_), channel_id=1, source_target_pairs={{0,1},{1,0},{2,3},{3,2},{4,5},{5,4},{6,7},{7,6},{8,9},{9,8},{10,11... | collective-permute-start | bytes 1572872 | tf_op jit(solution)/shard_map/ppermute | solution.py:18
  43.7 85.7 %copy-start.2 = (bf16[2,512,256]{2,1,0:T(8,128)(2,1)}, bf16[2,512,256]{2,1,0:T(8,128)(2,1)S(1)}, u32[]{:S(2)}) copy-start(bf16[2,512,256]{2,1,0:T(8,128)(2,1)S(1)} %collective-permute-done.15.refs_7_) | copy-start | bytes 1572868
  43.7 1.2 copy-start.4
  48.0 16.8 %copy-start.5 = (bf16[2,512,256]{2,1,0:T(8,128)(2,1)S(1)}, bf16[2,512,256]{2,1,0:T(8,128)(2,1)}, u32[]{:S(2)}) copy-start(bf16[2,512,256]{2,1,0:T(8,128)(2,1)} %copy-done.3) | copy-start | bytes 1572868
  48.0 23.8 %collective-permute-start.23 = (f16[2,128,896]{2,1,0:T(8,128)(2,1)S(1)}, f16[2,128,896]{2,1,0:T(8,128)(2,1)S(1)}, u32[]{:S(2)}, u32[]{:S(2)}) collective-permute-start(f16[2,128,896]{2,1,0:T(8,128)(2,1)S(1)} %fusion.7), channel_id=1, source_target_pairs={{0,16},{16,32},{32,48},{48,64},{64,80},{80,96},{96,112},{112,0},{1... | collective-permute-start | bytes 1376264 | tf_op jit(solution)/shard_map/ppermute | solution.py:29
  62.2 14.6 %collective-permute-start.2 = (f32[2,256,512]{2,1,0:T(8,128)}, f32[2,256,512]{2,1,0:T(8,128)S(1)}, u32[]{:S(2)}, u32[]{:S(2)}) collective-permute-start(f32[2,256,512]{2,1,0:T(8,128)} %get-tuple-element.10), channel_id=1, source_target_pairs={{0,2},{2,4},{4,6},{6,0},{1,7},{3,1},{5,3},{7,5},{8,10},{10,12},{12... | collective-permute-start | bytes 3145736 | tf_op jit(solution)/shard_map/ppermute | solution.py:29
  71.8 0.9 copy-start.7
  71.8 13.6 %copy-start = (f32[3,2,256,896]{3,2,1,0:T(8,128)}, f32[3,2,256,896]{3,2,1,0:T(8,128)S(1)}, u32[]{:S(2)}) copy-start(f32[3,2,256,896]{3,2,1,0:T(8,128)S(1)} %get-tuple-element.12) | copy-start | bytes 16515076
  71.9 4.9 %copy-start.12 = (f32[4,256,512]{2,1,0:T(8,128)S(1)}, f32[4,256,512]{2,1,0:T(8,128)}, u32[]{:S(2)}) copy-start(f32[4,256,512]{2,1,0:T(8,128)} %get-tuple-element.9) | copy-start | bytes 6291460
  72.7 12.6 %collective-permute-start.24 = (f16[2,256,896]{2,1,0:T(8,128)(2,1)S(1)}, f16[2,256,896]{2,1,0:T(8,128)(2,1)S(1)}, u32[]{:S(2)}, u32[]{:S(2)}) collective-permute-start(f16[2,256,896]{2,1,0:T(8,128)(2,1)S(1)} %fusion), channel_id=1, source_target_pairs={{0,16},{16,32},{32,48},{48,64},{64,80},{80,96},{96,112},{112,0},{1... | collective-permute-start | bytes 2752520 | tf_op jit(solution)/shard_map/ppermute | solution.py:29
  78.8 9.8 %copy-start.11 = (bf16[512,256]{1,0:T(8,128)(2,1)S(1)}, bf16[512,256]{1,0:T(8,128)(2,1)}, u32[]{:S(2)}) copy-start(bf16[512,256]{1,0:T(8,128)(2,1)} %get-tuple-element.23) | copy-start | bytes 786436
  78.8 40.5 %collective-permute-start.3 = (f32[4,256,512]{2,1,0:T(8,128)}, f32[4,256,512]{2,1,0:T(8,128)}, u32[]{:S(2)}, u32[]{:S(2)}) collective-permute-start(f32[4,256,512]{2,1,0:T(8,128)} %pad_maximum_fusion), channel_id=1, source_target_pairs={{0,2},{2,4},{4,6},{6,0},{1,7},{3,1},{5,3},{7,5},{8,10},{10,12},{12... | collective-permute-start | bytes 6291464 | tf_op jit(solution)/shard_map/ppermute | solution.py:29
  86.6 24.3 %collective-permute-start.25 = (f16[2,256,896]{2,1,0:T(8,128)(2,1)}, f16[2,256,896]{2,1,0:T(8,128)(2,1)S(1)}, u32[]{:S(2)}, u32[]{:S(2)}) collective-permute-start(f16[2,256,896]{2,1,0:T(8,128)(2,1)} %fusion.1), channel_id=1, source_target_pairs={{0,16},{16,32},{32,48},{48,64},{64,80},{80,96},{96,112},{112,0},{1... | collective-permute-start | bytes 2752520 | tf_op jit(solution)/shard_map/ppermute | solution.py:29
  88.5 1.5 collective-permute-start.16
  90.1 23.6 %copy-start.15 = (bf16[512,256]{1,0:T(8,128)(2,1)}, bf16[512,256]{1,0:T(8,128)(2,1)S(1)}, u32[]{:S(2)}) copy-start(bf16[512,256]{1,0:T(8,128)(2,1)S(1)} %collective-permute-done.16) | copy-start | bytes 786436
  90.1 20.7 %collective-permute-start.17 = (bf16[2,512,256]{2,1,0:T(8,128)(2,1)S(1)}, bf16[2,512,256]{2,1,0:T(8,128)(2,1)}, u32[]{:S(2)}, u32[]{:S(2)}) collective-permute-start(bf16[2,512,256]{2,1,0:T(8,128)(2,1)S(1)} %pad_maximum_fusion.6), channel_id=1, source_target_pairs={{0,2},{2,4},{4,6},{6,0},{1,7},{3,1},{5,3},{7,5},{8,10},{10,12},{12... | collective-permute-start | bytes 1572872 | tf_op jit(solution)/shard_map/ppermute | solution.py:29
  110.9 14.9 %collective-permute-start.18 = (bf16[2,512,256]{2,1,0:T(8,128)(2,1)}, bf16[2,512,256]{2,1,0:T(8,128)(2,1)}, u32[]{:S(2)}, u32[]{:S(2)}) collective-permute-start(bf16[2,512,256]{2,1,0:T(8,128)(2,1)} %collective-permute-done.17), channel_id=1, source_target_pairs={{0,1},{1,0},{2,3},{3,2},{4,5},{5,4},{6,7},{7,6},{8,9},{9,8},{10,11... | collective-permute-start | bytes 1572872 | tf_op jit(solution)/shard_map/ppermute | solution.py:18
  113.6 7.1 %copy-start.20 = (s32[16]{0:T(128)S(1)}, s32[16]{0:T(128)}, u32[]{:S(2)}) copy-start(s32[16]{0:T(128)} %constant.220.clone) | copy-start | bytes 196
  113.6 7.1 %copy-start.21 = (s32[16]{0:T(128)S(1)}, s32[16]{0:T(128)}, u32[]{:S(2)}) copy-start(s32[16]{0:T(128)} %constant.219.clone) | copy-start | bytes 196
  113.6 7.1 %copy-start.22 = (s32[16]{0:T(128)S(1)}, s32[16]{0:T(128)}, u32[]{:S(2)}) copy-start(s32[16]{0:T(128)} %constant.218.clone) | copy-start | bytes 196
  113.7 7.1 %copy-start.23 = (s32[16]{0:T(128)S(1)}, s32[16]{0:T(128)}, u32[]{:S(2)}) copy-start(s32[16]{0:T(128)} %constant.217.clone) | copy-start | bytes 196
  113.7 7.1 %copy-start.24 = (s32[16]{0:T(128)S(1)}, s32[16]{0:T(128)}, u32[]{:S(2)}) copy-start(s32[16]{0:T(128)} %constant.216.clone) | copy-start | bytes 196
  113.7 7.1 %copy-start.25 = (s32[16]{0:T(128)S(1)}, s32[16]{0:T(128)}, u32[]{:S(2)}) copy-start(s32[16]{0:T(128)} %constant.215.clone) | copy-start | bytes 196
  113.7 7.1 %copy-start.6 = (bf16[2,512,256]{2,1,0:T(8,128)(2,1)S(1)}, bf16[2,512,256]{2,1,0:T(8,128)(2,1)}, u32[]{:S(2)}) copy-start(bf16[2,512,256]{2,1,0:T(8,128)(2,1)} %copy-done.3) | copy-start | bytes 1572868
  113.7 14.2 %collective-permute-start.26 = (f16[2,256,896]{2,1,0:T(8,128)(2,1)}, f16[2,256,896]{2,1,0:T(8,128)(2,1)}, u32[]{:S(2)}, u32[]{:S(2)}) collective-permute-start(f16[2,256,896]{2,1,0:T(8,128)(2,1)} %fusion.2), channel_id=1, source_target_pairs={{0,16},{16,32},{32,48},{48,64},{64,80},{80,96},{96,112},{112,0},{1... | collective-permute-start | bytes 2752520 | tf_op jit(solution)/shard_map/ppermute | solution.py:29
  118.8 6.4 %collective-permute-start.19 = (bf16[512,256]{1,0:T(8,128)(2,1)}, bf16[512,256]{1,0:T(8,128)(2,1)}, u32[]{:S(2)}, u32[]{:S(2)}) collective-permute-start(bf16[512,256]{1,0:T(8,128)(2,1)} %get-tuple-element.19), channel_id=1, source_target_pairs={{0,2},{2,4},{4,6},{6,0},{1,7},{3,1},{5,3},{7,5},{8,10},{10,12},{12... | collective-permute-start | bytes 786440 | tf_op jit(solution)/shard_map/ppermute | solution.py:29
  120.6 11.0 %collective-permute-start.4 = (f32[2,256,512]{2,1,0:T(8,128)S(1)}, f32[2,256,512]{2,1,0:T(8,128)}, u32[]{:S(2)}, u32[]{:S(2)}) collective-permute-start(f32[2,256,512]{2,1,0:T(8,128)S(1)} %dynamic-slice_bitcast_fusion), channel_id=1, source_target_pairs={{0,1},{1,0},{2,3},{3,2},{4,5},{5,4},{6,7},{7,6},{8,9},{9,8},{10,11... | collective-permute-start | bytes 3145736 | tf_op jit(solution)/shard_map/ppermute | solution.py:18
  120.8 6.0 %copy-start.14 = (bf16[1,512,256]{2,1,0:T(8,128)(2,1)S(1)}, bf16[1,512,256]{2,1,0:T(8,128)(2,1)}, u32[]{:S(2)}) copy-start(bf16[1,512,256]{2,1,0:T(8,128)(2,1)} %get-tuple-element.20) | copy-start | bytes 786436
  120.9 30.5 %slice-start = ((s8[7340032]{0:T(1024)(128)(4,1)}), s8[4194304]{0:T(1024)(128)(4,1)S(1)}, s32[]{:S(2)}) async-start(s8[7340032]{0:T(1024)(128)(4,1)} %bitcast.55), calls=%async_computation | async-start | bytes 8388608
  124.2 5.0 %copy-start.16 = (bf16[512,256]{1,0:T(8,128)(2,1)S(1)}, bf16[512,256]{1,0:T(8,128)(2,1)}, u32[]{:S(2)}) copy-start(bf16[512,256]{1,0:T(8,128)(2,1)} %copy-done.15) | copy-start | bytes 786436
  125.2 4.0 %collective-permute-start.20 = (bf16[512,256]{1,0:T(8,128)(2,1)}, bf16[512,256]{1,0:T(8,128)(2,1)S(1)}, u32[]{:S(2)}, u32[]{:S(2)}) collective-permute-start(bf16[512,256]{1,0:T(8,128)(2,1)} %collective-permute-done.19), channel_id=1, source_target_pairs={{0,1},{1,0},{2,3},{3,2},{4,5},{5,4},{6,7},{7,6},{8,9},{9,8},{10,11... | collective-permute-start | bytes 786440 | tf_op jit(solution)/shard_map/ppermute | solution.py:18
  127.9 1.5 copy-start.10
  127.9 30.7 %collective-permute-start.27 = (f16[2,256,896]{2,1,0:T(8,128)(2,1)}, f16[2,256,896]{2,1,0:T(8,128)(2,1)S(1)}, u32[]{:S(2)}, u32[]{:S(2)}) collective-permute-start(f16[2,256,896]{2,1,0:T(8,128)(2,1)} %collective-permute-done.26), channel_id=1, source_target_pairs={{0,1},{1,0},{2,3},{3,2},{4,5},{5,4},{6,7},{7,6},{8,9},{9,8},{10,11... | collective-permute-start | bytes 2752520 | tf_op jit(solution)/shard_map/ppermute | solution.py:18
  129.2 22.2 %slice-start.1 = ((s8[7340032]{0:T(1024)(128)(4,1)}), s8[3145728]{0:T(1024)(128)(4,1)S(1)}, s32[]{:S(2)}) async-start(s8[7340032]{0:T(1024)(128)(4,1)} %bitcast.55), calls=%async_computation.1 | async-start | bytes 6291456
  129.4 2.1 %slice-start.2 = ((bf16[2,512,256]{2,1,0:T(8,128)(2,1)}), bf16[1,512,256]{2,1,0:T(8,128)(2,1)S(1)}, s32[]{:S(2)}) async-start(bf16[2,512,256]{2,1,0:T(8,128)(2,1)} %copy-done.2), calls=%async_computation.2 | async-start | bytes 524288 | tf_op jit(solution)/shard_map/slice | solution.py:264
  129.4 2.2 %copy-start.13 = (f32[2,256,512]{2,1,0:T(8,128)S(1)}, f32[2,256,512]{2,1,0:T(8,128)}, u32[]{:S(2)}) copy-start(f32[2,256,512]{2,1,0:T(8,128)} %get-tuple-element.8) | copy-start | bytes 3145732
  133.0 25.7 %copy-start.8 = (f32[256,896]{1,0:T(8,128)S(1)}, f32[256,896]{1,0:T(8,128)}, u32[]{:S(2)}) copy-start(f32[256,896]{1,0:T(8,128)} %copy-done.7) | copy-start | bytes 2752516
  133.0 30.7 %collective-permute-start.5 = (f32[256,512]{1,0:T(8,128)S(1)}, f32[256,512]{1,0:T(8,128)S(1)}, u32[]{:S(2)}, u32[]{:S(2)}) collective-permute-start(f32[256,512]{1,0:T(8,128)S(1)} %fusion.3), channel_id=1, source_target_pairs={{0,8},{8,0},{1,9},{9,1},{2,10},{10,2},{3,11},{11,3},{4,12},{12,4},... | collective-permute-start | bytes 1572872 | tf_op jit(solution)/shard_map/ppermute | solution.py:18
  (1 other events, 0.8 us)

commit v3 on v2

--- a/solution.py
+++ b/solution.py
@@ -56,7 +56,7 @@
     n, r = order.shape[0], 256
 
     def kernel(order_ref, h_ref, hc_ref, w_ref, wc_ref, *rest):
-        outs, (h_t, rows, sums, sems, out_sems) = rest[:3], rest[3:]
+        outs, (h_t, rows, sums, sems, out_sems) = rest[:4], rest[4:]
 
         def fetch(i):
             at = pl.ds(pl.multiple_of(order_ref[i] * r, r), r)
@@ -82,8 +82,8 @@
     return pl.pallas_call(
         kernel,
         in_specs=[pl.BlockSpec(memory_space=pltpu.SMEM), vmem, vmem, hbm, hbm],
-        out_specs=[hbm] * 3,
-        out_shape=[jax.ShapeDtypeStruct((k, r, t), F32) for k in (2, 4, 2)],
+        out_specs=[hbm] * 4,
+        out_shape=[jax.ShapeDtypeStruct((k, r, t), F32) for k in (2, 2, 2, 2)],
         scratch_shapes=[
             VMEM((2, u, t), BF16),
             VMEM((n, 2, r, u), BF16),
@@ -188,7 +188,7 @@
             scratch_shapes=[VMEM((t, u), F32)],
         ),
         out_shape=jax.ShapeDtypeStruct((t, u), BF16),
-        compiler_params=pltpu.CompilerParams(vmem_limit_bytes=14 << 20),
+        compiler_params=pltpu.CompilerParams(vmem_limit_bytes=57 << 20),
         cost_estimate=cost(2 * m * n * t * r * u, 2 * m * n * (t * r + r * u)),
         name="hidden_gradient",
     )(order, *blocks, *([weight] * m))
@@ -196,7 +196,6 @@
 
 def layer(hidden, weight, cotangent):
     tokens, _ = hidden.shape
-    rows = cotangent.shape[1]
     scale = float(tokens * 16) ** -0.5
     yh, z, yl, x, c = (lax.axis_index(a) for a in (YH, Z, YL, X, C))
 
@@ -226,20 +225,25 @@
 
     ahead = 1 - 2 * c
     at_x = x + table([2, 2, 0, 0, 0, 0, 0, 0]) + ahead * table([0, 0, 1, 1, 1, 1, 0, 0])
-    at_y = c * table([1, 1, 1, 1, 0, 0, 0, 0]) + (1 - c) * table([0, 0, 0, 0, 1, 1, 0, 0])
-    at_y += yl * table([0, 0, 0, 0, 0, 0, 1, 0]) + (1 - yl) * table([0, 0, 0, 0, 0, 0, 0, 1])
+    at_y = c * table([1, 1, 0, 0, 0, 0, 0, 0]) + yl * table([0, 0, 0, 0, 1, 1, 0, 1])
+    at_y += (1 - yl) * table([0, 0, 1, 1, 0, 0, 1, 0])
     at_c = table([0, 1, 0, 1, 0, 1, 0, 0]) + c * table([0, 0, 0, 0, 0, 0, 1, 1])
     order = at_y * 8 + at_x % 4 * 2 + at_c
-    first, following, last = out_parts(hidden, hidden_c, weight, weight_c, order)
+    first, give2, keep2, last = out_parts(hidden, hidden_c, weight, weight_c, order)
     came = x_out(first)
-    came = x_out(jnp.concatenate([following[:2] + came, following[2:]], 0))
-    came = came.reshape(2, 2, rows, tokens)
-    for_other = lax.dynamic_index_in_dim(came, 1 - c, 1, keepdims=False)
-    from_other = other_core(for_other)
-    for_own = lax.dynamic_index_in_dim(came, c, 1, keepdims=False)
-    keep = last[0] + (pick(for_own, (yl + c) % 2) + pick(from_other, (yl + 1 + c) % 2))
-    give = last[1] + (pick(for_own, (yl + 1 + c) % 2) + pick(from_other, (yl + c) % 2))
+    gives = (yl != c).astype(F32)
+    far_give = x_out(give2 + came * gives)
+    far_keep = x_out(keep2 + came * (1.0 - gives))
+
+    def both_cores(array):
+        other = other_core(pick(array, 1 - c))
+        return pick(array, c) + other
+
+    give = both_cores(far_give)
+    give = last[0] + give
     given = other_yl(give)
+    keep = both_cores(far_keep)
+    keep = last[1] + keep
     output = (keep + given).T.astype(BF16)
 
     blocks = [crit, crit_c, a1, a2, b2, b1, a3, b3]

time: 166 us -> 160 us (0.964)
  waiting for transfers between devices: 48.3 us -> 34 us
  other arithmetic: 14.7 us -> 21.7 us
  local copies, waits for them, and re-layouts: 13.9 us -> 10.9 us
  Pallas kernels: 25.6 us -> 28.1 us
  starting transfers between devices: 62.1 us -> 63.8 us
    ppermute x11 -> x12, waiting for transfers between devices: 31.4 us -> 21 us  [move(): return lax.ppermute(array, (axis, C), flat)]
    ppermute x15 -> x16, waiting for transfers between devices: 12.2 us -> 8.27 us  [move(): return lax.ppermute(array, axis, [(i, (i + by) % n) for i in range(n)])]
    pallas_call x1, Pallas kernels: 7.26 us -> 9.57 us  [hidden_gradient(): pl.pallas_call(kernel, grid_spec=pltpu.PrefetchScalarGridSpec(num_scalar_...]
    slice x5 -> x4, local copies, waits for them, and re-layouts: 4.1 us -> 1.97 us  [layer(): theirs = jnp.stack([crit_c[0], a2[0], b1[0], b3[0]])]
    ppermute x15 -> x16, starting transfers between devices: 34.3 us -> 36.3 us  [move(): return lax.ppermute(array, axis, [(i, (i + by) % n) for i in range(n)])]
    convert_element_type x1, other arithmetic: 1.26 us -> 2.98 us  [layer(): came = z_out((g[1] * 0.25 + came.astype(F32)).astype(F16))]
    add x2, other arithmetic: 1.71 us -> 3.39 us  [the longest x1 3.24 us: layer(): far_keep = x_out(keep2 + came * (1.0 - gives))]
    unnamed x73 -> x63, local copies, waits for them, and re-layouts: 3.45 us -> 3.88 us
  transfers between devices with their start and end apart: 28 -> 30, of which waited for: 13 -> 13; matrix products, arithmetic and copies ran while one was open for 13% -> 18% of each run, Pallas kernels for 15% -> 18%
where the time goes in v3:
time: 160 us; the launch traced here: 159 us
  starting transfers between devices  63.8 us (40%)
  waiting for transfers between devices  34 us (21%)
  Pallas kernels  28.1 us (18%)
  other arithmetic  21.7 us (14%)
  local copies, waits for them, and re-layouts  10.9 us (7%)
    ppermute x16, starting transfers between devices, move(): return lax.ppermute(array, axis, [(i, (i + by) % n) for i in range(n)])  36.3 us
    ppermute x12, starting transfers between devices, move(): return lax.ppermute(array, (axis, C), flat)  25.5 us
    ppermute x12, waiting for transfers between devices, move(): return lax.ppermute(array, (axis, C), flat)  21 us
    pallas_call x2, Pallas kernels, grad_parts(): pl.pallas_call(kernel, in_specs=[pl.BlockSpec(memory_space=pltpu.SMEM)] +...  10.1 us
    pallas_call x1, Pallas kernels, hidden_gradient(): pl.pallas_call(kernel, grid_spec=pltpu.PrefetchScalarGridSpec(num_scalar_...  9.57 us
    pallas_call x1, Pallas kernels, out_parts(): pl.pallas_call(kernel, in_specs=[pl.BlockSpec(memory_space=pltpu.SMEM), v...  8.39 us
    ppermute x16, waiting for transfers between devices, move(): return lax.ppermute(array, axis, [(i, (i + by) % n) for i in range(n)])  8.27 us
    ppermute x1, waiting for transfers between devices, layer(): far = lax.ppermute(cotangent, (YH, YL), [(2, 0), (1, 3)])  4.67 us
  transfers between devices with their start and end apart: 30, of which 13 were waited for; matrix products, arithmetic and copies ran while one was open for 18% of the time, Pallas kernels for 18%

profile of v3, /device:TPU:1, one launch (start us, length us, event | category | flops | bytes accessed | tf_op | source)
XLA Modules:
  0.0 159.4 jit_solution(8391319029301101467)
XLA Ops:
  0.7 3.3 %collective-permute-start.1 = (bf16[4096,896]{1,0:T(8,128)(2,1)}, bf16[4096,896]{1,0:T(8,128)(2,1)}, u32[]{:S(2)}, u32[]{:S(2)}) collective-permute-start(bf16[4096,896]{1,0:T(8,128)(2,1)} %refs_7_.1), channel_id=1, source_target_pairs={{0,1},{1,0},{2,3},{3,2},{4,5},{5,4},{6,7},{7,6},{8,9},{9,8},{10,11... | collective-permute-start | bytes 22020104 | tf_op jit(solution)/shard_map/ppermute | solution.py:18
  4.0 1.3 collective-permute-start.9
  5.3 0.7 collective-permute-start.10
  5.9 5.8 %collective-permute-start.23 = (bf16[512,896]{1,0:T(8,128)(2,1)}, bf16[512,896]{1,0:T(8,128)(2,1)}, u32[]{:S(2)}, u32[]{:S(2)}) collective-permute-start(bf16[512,896]{1,0:T(8,128)(2,1)} %refs_8_.3), channel_id=1, source_target_pairs={{0,128},{128,0},{1,129},{129,1},{2,130},{130,2},{3,131},{131,3},{4... | collective-permute-start | bytes 2752520 | tf_op jit(solution)/shard_map/ppermute | solution.py:18
  11.7 0.2 collective-permute-done.8
  11.9 1.7 %broadcast_select_fusion = (bf16[512,256]{1,0:T(8,128)(2,1)}, bf16[1,512,256]{2,1,0:T(8,128)(2,1)S(1)}) fusion(bf16[512,256]{1,0:T(8,128)(2,1)S(1)} %collective-permute-done.8, bf16[512,256]{1,0:T(8,128)(2,1)} %param.21, pred[]{:T(512)S(6)} %eq.30), kind=kLoop, calls=%fused_computation.30 | loop fusion | flops 262144 | bytes 1048577 | tf_op jit(solution)/shard_map/jit(_where)/select_n | solution.py:211
  13.6 4.7 %collective-permute-done.9 = bf16[512,256]{1,0:T(8,128)(2,1)S(1)} collective-permute-done((bf16[512,256]{1,0:T(8,128)(2,1)}, bf16[512,256]{1,0:T(8,128)(2,1)S(1)}, u32[]{:S(2)}, u32[]{:S(2)}) %collective-permute-start.9) | collective-permute-done | bytes 262176 | tf_op jit(solution)/shard_map/ppermute | solution.py:202
  18.4 1.6 %collective-permute-start.12 = (bf16[2,512,256]{2,1,0:T(8,128)(2,1)S(1)}, bf16[2,512,256]{2,1,0:T(8,128)(2,1)S(1)}, u32[]{:S(2)}, u32[]{:S(2)}) collective-permute-start(bf16[2,512,256]{2,1,0:T(8,128)(2,1)S(1)} %pad_maximum_fusion.4.refs_0_), channel_id=1, source_target_pairs={{0,1},{1,0},{2,3},{3,2},{4,5},{5,4},{6,7},{7,6},{8,9},{9,8},{10,11... | collective-permute-start | bytes 1572872 | tf_op jit(solution)/shard_map/ppermute | solution.py:18
  20.0 2.5 %collective-permute-start.11 = (bf16[2,512,256]{2,1,0:T(8,128)(2,1)S(1)}, bf16[2,512,256]{2,1,0:T(8,128)(2,1)}, u32[]{:S(2)}, u32[]{:S(2)}) collective-permute-start(bf16[2,512,256]{2,1,0:T(8,128)(2,1)S(1)} %pad_maximum_fusion.4.refs_0_), channel_id=1, source_target_pairs={{0,2},{2,4},{4,6},{6,0},{1,7},{3,1},{5,3},{7,5},{8,10},{10,12},{12... | collective-permute-start | bytes 1572872 | tf_op jit(solution)/shard_map/ppermute | solution.py:29
  22.5 1.5 collective-permute-start.13
  24.0 0.8 copy-done.2
  24.8 3.8 %collective-permute-done.11.refs_2_ = bf16[2,512,256]{2,1,0:T(8,128)(2,1)} collective-permute-done((bf16[2,512,256]{2,1,0:T(8,128)(2,1)S(1)}, bf16[2,512,256]{2,1,0:T(8,128)(2,1)}, u32[]{:S(2)}, u32[]{:S(2)}) %collective-permute-start.11) | collective-permute-done | bytes 524320 | tf_op jit(solution)/shard_map/ppermute | solution.py:29
  28.6 3.5 %collective-permute-start.15 = (bf16[2,512,256]{2,1,0:T(8,128)(2,1)}, bf16[2,512,256]{2,1,0:T(8,128)(2,1)}, u32[]{:S(2)}, u32[]{:S(2)}) collective-permute-start(bf16[2,512,256]{2,1,0:T(8,128)(2,1)} %collective-permute-done.11.refs_2_), channel_id=1, source_target_pairs={{0,2},{2,4},{4,6},{6,0},{1,7},{3,1},{5,3},{7,5},{8,10},{10,12},{12... | collective-permute-start | bytes 1572872 | tf_op jit(solution)/shard_map/ppermute | solution.py:29
  32.1 5.9 %collective-permute-done.23.refs_9_ = bf16[512,896]{1,0:T(8,128)(2,1)} collective-permute-done((bf16[512,896]{1,0:T(8,128)(2,1)}, bf16[512,896]{1,0:T(8,128)(2,1)}, u32[]{:S(2)}, u32[]{:S(2)}) %collective-permute-start.23) | collective-permute-done | bytes 917536 | tf_op jit(solution)/shard_map/ppermute | solution.py:18
  38.1 1.0 collective-permute-start.24
  39.0 0.5 collective-permute-start.14
  39.5 0.4 collective-permute-done.15.refs_6_
  39.9 1.9 %collective-permute-start.17 = (bf16[2,512,256]{2,1,0:T(8,128)(2,1)}, bf16[2,512,256]{2,1,0:T(8,128)(2,1)S(1)}, u32[]{:S(2)}, u32[]{:S(2)}) collective-permute-start(bf16[2,512,256]{2,1,0:T(8,128)(2,1)} %collective-permute-done.15.refs_6_), channel_id=1, source_target_pairs={{0,1},{1,0},{2,3},{3,2},{4,5},{5,4},{6,7},{7,6},{8,9},{9,8},{10,11... | collective-permute-start | bytes 1572872 | tf_op jit(solution)/shard_map/ppermute | solution.py:18
  41.9 0.3 collective-permute-done.16.refs_5_
  42.2 0.6 collective-permute-done.14.refs_4_
  42.8 0.7 collective-permute-done.17.refs_7_
  43.6 1.0 copy-done.3
  44.6 3.0 %grad_parts.3 = f32[1,2,128,896]{3,2,1,0:T(8,128)S(1)} custom-call(s32[8]{0:T(128)S(1)} %multiply_add_fusion.2.table_ref, bf16[2,512,256]{2,1,0:T(8,128)(2,1)S(1)} %pad_maximum_fusion.4.refs_0_, bf16[2,512,256]{2,1,0:T(8,128)(2,1)S(1)} %copy-done.3, bf16[2,512,256]{2,1,0:T(8,128)(2,1)} %collective-permute-done.11.refs_2_, ...), custom_call_target="tpu_custom_call" | custom-call | flops 469762048 | bytes 1835008 | tf_op jit(solution)/shard_map/grad_parts/pallas_call | solution.py:141
  47.7 5.7 %collective-permute-start.25 = (f16[2,128,896]{2,1,0:T(8,128)(2,1)S(1)}, f16[2,128,896]{2,1,0:T(8,128)(2,1)S(1)}, u32[]{:S(2)}, u32[]{:S(2)}) collective-permute-start(f16[2,128,896]{2,1,0:T(8,128)(2,1)S(1)} %fusion.7), channel_id=1, source_target_pairs={{0,16},{16,32},{32,48},{48,64},{64,80},{80,96},{96,112},{112,0},{1... | collective-permute-start | bytes 1376264 | tf_op jit(solution)/shard_map/ppermute | solution.py:29
  53.3 7.2 %grad_parts.2 = (f32[3,2,256,896]{3,2,1,0:T(8,128)S(1)}, f32[256,896]{1,0:T(8,128)S(1)}) custom-call(s32[8]{0:T(128)S(1)} %multiply_add_fusion.2.table_ref, bf16[2,512,256]{2,1,0:T(8,128)(2,1)S(1)} %pad_maximum_fusion.4.refs_0_, bf16[2,512,256]{2,1,0:T(8,128)(2,1)S(1)} %copy-done.3, bf16[2,512,256]{2,1,0:T(8,128)(2,1)} %collective-permute-done.11.refs_2_, ...), custom_call_target="tpu_custom_call" | custom-call | flops 3288334336 | bytes 12845056 | tf_op jit(solution)/shard_map/grad_parts/pallas_call | solution.py:141
  60.8 1.7 %fusion = f16[2,256,896]{2,1,0:T(8,128)(2,1)} fusion(f32[2,128,896]{2,1,0:T(8,128)S(1)} %get-tuple-element.28, f32[2,128,896]{2,1,0:T(8,128)S(1)} %get-tuple-element.27, f32[3,2,256,896]{3,2,1,0:T(8,128)S(1)} %get-tuple-element.14), kind=kLoop, calls=%fused_computation.1 | loop fusion | flops 1835008 | bytes 4587520 | tf_op jit(solution)/shard_map/convert_element_type | solution.py:261
  62.5 0.8 copy-done
  63.3 0.2 copy-done.5
  63.5 0.7 collective-permute-start.26
  64.3 8.4 %out_parts.1 = (f32[2,256,512]{2,1,0:T(8,128)}, f32[2,256,512]{2,1,0:T(8,128)}, f32[2,256,512]{2,1,0:T(8,128)}, f32[2,256,512]{2,1,0:T(8,128)}) custom-call(s32[8]{0:T(128)S(1)} %fusion.12.order_ref, bf16[512,896]{1,0:T(8,128)(2,1)S(1)} %copy-done.1, bf16[512,896]{1,0:T(8,128)(2,1)S(1)} %collective-permute-done.hc_ref.refs_10_, bf16[4096,896]{1,0:T(8,128)(2,1)} %refs_7_.1, ...), custom_call_target="tpu_custom_call" | custom-call | flops 3758096384 | bytes 4194304 | tf_op jit(solution)/shard_map/out_parts/pallas_call | solution.py:82
  72.7 2.5 %collective-permute-start.2 = (f32[2,256,512]{2,1,0:T(8,128)}, f32[2,256,512]{2,1,0:T(8,128)}, u32[]{:S(2)}, u32[]{:S(2)}) collective-permute-start(f32[2,256,512]{2,1,0:T(8,128)} %get-tuple-element.11), channel_id=1, source_target_pairs={{0,2},{2,4},{4,6},{6,0},{1,7},{3,1},{5,3},{7,5},{8,10},{10,12},{12... | collective-permute-start | bytes 3145736 | tf_op jit(solution)/shard_map/ppermute | solution.py:29
  75.3 1.1 collective-permute-done.26
  76.4 3.0 %fusion.1 = f16[2,256,896]{2,1,0:T(8,128)(2,1)} fusion(f16[2,256,896]{2,1,0:T(8,128)(2,1)} %collective-permute-done.26, f32[3,2,256,896]{3,2,1,0:T(8,128)} %copy-done), kind=kLoop, calls=%fused_computation.3 | loop fusion | flops 1835008 | bytes 3670016 | tf_op jit(solution)/shard_map/convert_element_type | solution.py:262
  79.4 1.9 %collective-permute-start.27 = (f16[2,256,896]{2,1,0:T(8,128)(2,1)}, f16[2,256,896]{2,1,0:T(8,128)(2,1)}, u32[]{:S(2)}, u32[]{:S(2)}) collective-permute-start(f16[2,256,896]{2,1,0:T(8,128)(2,1)} %fusion.1), channel_id=1, source_target_pairs={{0,16},{16,32},{32,48},{48,64},{64,80},{80,96},{96,112},{112,0},{1... | collective-permute-start | bytes 2752520 | tf_op jit(solution)/shard_map/ppermute | solution.py:29
  81.4 2.3 %collective-permute-start.19 = (bf16[2,512,256]{2,1,0:T(8,128)(2,1)S(1)}, bf16[2,512,256]{2,1,0:T(8,128)(2,1)}, u32[]{:S(2)}, u32[]{:S(2)}) collective-permute-start(bf16[2,512,256]{2,1,0:T(8,128)(2,1)S(1)} %pad_maximum_fusion.5), channel_id=1, source_target_pairs={{0,2},{2,4},{4,6},{6,0},{1,7},{3,1},{5,3},{7,5},{8,10},{10,12},{12... | collective-permute-start | bytes 1572872 | tf_op jit(solution)/shard_map/ppermute | solution.py:29
  83.6 9.2 %collective-permute-done.19 = bf16[2,512,256]{2,1,0:T(8,128)(2,1)} collective-permute-done((bf16[2,512,256]{2,1,0:T(8,128)(2,1)S(1)}, bf16[2,512,256]{2,1,0:T(8,128)(2,1)}, u32[]{:S(2)}, u32[]{:S(2)}) %collective-permute-start.19) | collective-permute-done | bytes 524320 | tf_op jit(solution)/shard_map/ppermute | solution.py:29
  92.9 3.2 %multiply_add_fusion.1 = (f32[2,256,512]{2,1,0:T(8,128)}, f32[2,256,512]{2,1,0:T(8,128)}) fusion(f32[2,256,512]{2,1,0:T(8,128)} %get-tuple-element.10, f32[2,256,512]{2,1,0:T(8,128)} %collective-permute-done.2, f32[]{:T(128)S(6)} %sub.27, f32[2,256,512]{2,1,0:T(8,128)S(1)} %copy-done.11, f32[]{:T(128)S(6)} %convert_element_type.41), kind=kLoop, calls=%fused_computation.13 | loop fusion | flops 1048576 | bytes 5242888 | tf_op jit(solution)/shard_map/add | solution.py:236
  96.2 3.8 %collective-permute-start.5 = (f32[2,256,512]{2,1,0:T(8,128)}, f32[2,256,512]{2,1,0:T(8,128)S(1)}, u32[]{:S(2)}, u32[]{:S(2)}) collective-permute-start(f32[2,256,512]{2,1,0:T(8,128)} %get-tuple-element.19), channel_id=1, source_target_pairs={{0,2},{2,4},{4,6},{6,0},{1,7},{3,1},{5,3},{7,5},{8,10},{10,12},{12... | collective-permute-start | bytes 3145736 | tf_op jit(solution)/shard_map/ppermute | solution.py:29
  100.0 3.0 %fusion.2 = f16[2,256,896]{2,1,0:T(8,128)(2,1)} fusion(f16[2,256,896]{2,1,0:T(8,128)(2,1)} %collective-permute-done.27, f32[3,2,256,896]{3,2,1,0:T(8,128)} %copy-done), kind=kLoop, calls=%fused_computation.5 | loop fusion | flops 1835008 | bytes 3670016 | tf_op jit(solution)/shard_map/convert_element_type | solution.py:263
  103.0 0.4 collective-permute-start.28
  103.4 1.9 %fusion.21 = (bf16[1,512,256]{2,1,0:T(8,128)(2,1)S(1)}, bf16[512,256]{1,0:T(8,128)(2,1)}, bf16[1,512,256]{2,1,0:T(8,128)(2,1)}) fusion(bf16[2,512,256]{2,1,0:T(8,128)(2,1)} %collective-permute-done.19), kind=kLoop, calls=%fused_computation.67 | loop fusion | bytes 1310720 | tf_op jit(solution)/shard_map/slice | solution.py:270
  105.3 0.4 collective-permute-start.21
  105.7 0.3 collective-permute-start.3
  106.0 0.5 fusion.15.order_ref
  106.5 1.0 slice.73
  107.5 1.0 slice.77
  108.5 1.0 slice.78
  109.5 1.0 slice.75
  110.5 4.4 %collective-permute-done.21 = bf16[512,256]{1,0:T(8,128)(2,1)} collective-permute-done((bf16[512,256]{1,0:T(8,128)(2,1)}, bf16[512,256]{1,0:T(8,128)(2,1)}, u32[]{:S(2)}, u32[]{:S(2)}) %collective-permute-start.21) | collective-permute-done | bytes 262176 | tf_op jit(solution)/shard_map/ppermute | solution.py:29
  114.9 1.8 %collective-permute-start.22 = (bf16[512,256]{1,0:T(8,128)(2,1)}, bf16[512,256]{1,0:T(8,128)(2,1)S(1)}, u32[]{:S(2)}, u32[]{:S(2)}) collective-permute-start(bf16[512,256]{1,0:T(8,128)(2,1)} %collective-permute-done.21), channel_id=1, source_target_pairs={{0,1},{1,0},{2,3},{3,2},{4,5},{5,4},{6,7},{7,6},{8,9},{9,8},{10,11... | collective-permute-start | bytes 786440 | tf_op jit(solution)/shard_map/ppermute | solution.py:18
  116.7 1.1 fusion.22
  117.8 2.1 %pad_maximum_fusion.2.refs_2_ = bf16[4,512,256]{2,1,0:T(8,128)(2,1)} fusion(bf16[1,512,256]{2,1,0:T(8,128)(2,1)} %bitcast.12, bf16[1,512,256]{2,1,0:T(8,128)(2,1)S(1)} %get-tuple-element.24, bf16[1,512,256]{2,1,0:T(8,128)(2,1)S(1)} %copy-done.12, bf16[1,512,256]{2,1,0:T(8,128)(2,1)S(1)} %bitcast.51), kind=kLoop, calls=%fused_computation.10 | loop fusion | flops 1572864 | bytes 2097152 | tf_op jit(solution)/shard_map/stack | solution.py:269
  120.1 1.1 pad_maximum_fusion.3.refs_3_
  121.2 0.6 collective-permute-start.29
  121.8 1.1 pad_maximum_fusion.refs_0_
  122.9 1.1 pad_maximum_fusion.1.refs_1_
  124.1 2.1 %collective-permute-done.3 = f32[2,256,512]{2,1,0:T(8,128)S(1)} collective-permute-done((f32[2,256,512]{2,1,0:T(8,128)}, f32[2,256,512]{2,1,0:T(8,128)S(1)}, u32[]{:S(2)}, u32[]{:S(2)}) %collective-permute-start.3) | collective-permute-done | bytes 1048608 | tf_op jit(solution)/shard_map/ppermute | solution.py:29
  126.1 1.8 %collective-permute-start.4 = (f32[256,512]{1,0:T(8,128)S(1)}, f32[256,512]{1,0:T(8,128)S(1)}, u32[]{:S(2)}, u32[]{:S(2)}) collective-permute-start(f32[256,512]{1,0:T(8,128)S(1)} %dynamic-slice_bitcast_fusion.1), channel_id=1, source_target_pairs={{0,1},{1,0},{2,3},{3,2},{4,5},{5,4},{6,7},{7,6},{8,9},{9,8},{10,11... | collective-permute-start | bytes 1572872 | tf_op jit(solution)/shard_map/ppermute | solution.py:18
  128.1 18.0 %collective-permute-start.7 = (f32[256,512]{1,0:T(8,128)S(1)}, f32[256,512]{1,0:T(8,128)S(1)}, u32[]{:S(2)}, u32[]{:S(2)}) collective-permute-start(f32[256,512]{1,0:T(8,128)S(1)} %fusion.3), channel_id=1, source_target_pairs={{0,8},{8,0},{1,9},{9,1},{2,10},{10,2},{3,11},{11,3},{4,12},{12,4},... | collective-permute-start | bytes 1572872 | tf_op jit(solution)/shard_map/ppermute | solution.py:18
  146.1 9.6 %hidden_gradient.1 = bf16[512,896]{1,0:T(8,128)(2,1)} custom-call(s32[16]{0:T(128)} %fusion.15.order_ref, bf16[4,512,256]{2,1,0:T(8,128)(2,1)} %pad_maximum_fusion.refs_0_, bf16[4,512,256]{2,1,0:T(8,128)(2,1)} %pad_maximum_fusion.1.refs_1_, bf16[4,512,256]{2,1,0:T(8,128)(2,1)} %pad_maximum_fusion.2.refs_2_, bf16[4,512,256]{2,1,0:T(8,128)(2,1)} %pad_maximum_fusion.3.refs_3_, ...), custom_call_target="tpu_custom_call" | custom-call | flops 3758096384 | bytes 11534336 | tf_op jit(solution)/shard_map/hidden_gradient/pallas_call | solution.py:181
  155.7 2.3 %bitcast_add_fusion.2 = f32[256,896]{1,0:T(8,128)} fusion(f32[256,896]{1,0:T(8,128)S(1)} %copy-done.6, f16[2,256,896]{2,1,0:T(8,128)(2,1)} %collective-permute-done.29, f16[2,256,896]{2,1,0:T(8,128)(2,1)} %collective-permute-done.28), kind=kLoop, calls=%fused_computation.14 | loop fusion | flops 1376256 | bytes 2752512 | tf_op jit(solution)/shard_map/add | solution.py:265
  158.0 0.4 collective-permute-done.7
  158.3 0.2 fusion.8
  158.6 0.8 copy.22
  (94 shorter events, 1.0 us)
Async XLA Ops:
  0.6 41.2 %copy-start.15 = (s32[8]{0:T(128)S(1)}, s32[8]{0:T(128)}, u32[]{:S(2)}) copy-start(s32[8]{0:T(128)} %constant.153.clone) | copy-start | bytes 100
  0.6 41.2 %copy-start.16 = (s32[8]{0:T(128)S(1)}, s32[8]{0:T(128)}, u32[]{:S(2)}) copy-start(s32[8]{0:T(128)} %constant.152.clone) | copy-start | bytes 100
  0.7 41.2 %copy-start.17 = (s32[8]{0:T(128)S(1)}, s32[8]{0:T(128)}, u32[]{:S(2)}) copy-start(s32[8]{0:T(128)} %constant.151.clone) | copy-start | bytes 100
  0.7 21.8 %copy-start.1 = (bf16[512,896]{1,0:T(8,128)(2,1)S(1)}, bf16[512,896]{1,0:T(8,128)(2,1)}, u32[]{:S(2)}) copy-start(bf16[512,896]{1,0:T(8,128)(2,1)} %refs_8_.3) | copy-start | bytes 2752516
  0.7 63.7 %collective-permute-start.1 = (bf16[4096,896]{1,0:T(8,128)(2,1)}, bf16[4096,896]{1,0:T(8,128)(2,1)}, u32[]{:S(2)}, u32[]{:S(2)}) collective-permute-start(bf16[4096,896]{1,0:T(8,128)(2,1)} %refs_7_.1), channel_id=1, source_target_pairs={{0,1},{1,0},{2,3},{3,2},{4,5},{5,4},{6,7},{7,6},{8,9},{9,8},{10,11... | collective-permute-start | bytes 22020104 | tf_op jit(solution)/shard_map/ppermute | solution.py:18
  4.0 8.0 %collective-permute-start.8 = (bf16[512,256]{1,0:T(8,128)(2,1)}, bf16[512,256]{1,0:T(8,128)(2,1)S(1)}, u32[]{:S(2)}, u32[]{:S(2)}) collective-permute-start(bf16[512,256]{1,0:T(8,128)(2,1)} %param.21), channel_id=1, source_target_pairs={{0,8},{8,0},{1,9},{9,1},{2,10},{10,2},{3,11},{11,3},{4,12},{12,4},... | collective-permute-start | bytes 786440 | tf_op jit(solution)/shard_map/ppermute | solution.py:18
  4.0 14.3 %collective-permute-start.9 = (bf16[512,256]{1,0:T(8,128)(2,1)}, bf16[512,256]{1,0:T(8,128)(2,1)S(1)}, u32[]{:S(2)}, u32[]{:S(2)}) collective-permute-start(bf16[512,256]{1,0:T(8,128)(2,1)} %param.21), channel_id=1, source_target_pairs={{128,0},{8,136},{129,1},{9,137},{130,2},{10,138},{131,3},{11,139},... | collective-permute-start | bytes 786440 | tf_op jit(solution)/shard_map/ppermute | solution.py:202
  5.3 13.0 %collective-permute-start.10 = (bf16[512,256]{1,0:T(8,128)(2,1)}, bf16[512,256]{1,0:T(8,128)(2,1)S(1)}, u32[]{:S(2)}, u32[]{:S(2)}) collective-permute-start(bf16[512,256]{1,0:T(8,128)(2,1)} %param.21), channel_id=1, source_target_pairs={{128,8},{8,128},{129,9},{9,129},{130,10},{10,130},{131,11},{11,131... | collective-permute-start | bytes 786440 | tf_op jit(solution)/shard_map/ppermute | solution.py:203
  5.9 32.1 %collective-permute-start.23 = (bf16[512,896]{1,0:T(8,128)(2,1)}, bf16[512,896]{1,0:T(8,128)(2,1)}, u32[]{:S(2)}, u32[]{:S(2)}) collective-permute-start(bf16[512,896]{1,0:T(8,128)(2,1)} %refs_8_.3), channel_id=1, source_target_pairs={{0,128},{128,0},{1,129},{129,1},{2,130},{130,2},{3,131},{131,3},{4... | collective-permute-start | bytes 2752520 | tf_op jit(solution)/shard_map/ppermute | solution.py:18
  13.6 6.4 %copy-start.7 = (bf16[1,512,256]{2,1,0:T(8,128)(2,1)}, bf16[1,512,256]{2,1,0:T(8,128)(2,1)S(1)}, u32[]{:S(2)}) copy-start(bf16[1,512,256]{2,1,0:T(8,128)(2,1)S(1)} %get-tuple-element.26) | copy-start | bytes 786436
  18.4 4.1 %collective-permute-start.12 = (bf16[2,512,256]{2,1,0:T(8,128)(2,1)S(1)}, bf16[2,512,256]{2,1,0:T(8,128)(2,1)S(1)}, u32[]{:S(2)}, u32[]{:S(2)}) collective-permute-start(bf16[2,512,256]{2,1,0:T(8,128)(2,1)S(1)} %pad_maximum_fusion.4.refs_0_), channel_id=1, source_target_pairs={{0,1},{1,0},{2,3},{3,2},{4,5},{5,4},{6,7},{7,6},{8,9},{9,8},{10,11... | collective-permute-start | bytes 1572872 | tf_op jit(solution)/shard_map/ppermute | solution.py:18
  20.0 8.6 %collective-permute-start.11 = (bf16[2,512,256]{2,1,0:T(8,128)(2,1)S(1)}, bf16[2,512,256]{2,1,0:T(8,128)(2,1)}, u32[]{:S(2)}, u32[]{:S(2)}) collective-permute-start(bf16[2,512,256]{2,1,0:T(8,128)(2,1)S(1)} %pad_maximum_fusion.4.refs_0_), channel_id=1, source_target_pairs={{0,2},{2,4},{4,6},{6,0},{1,7},{3,1},{5,3},{7,5},{8,10},{10,12},{12... | collective-permute-start | bytes 1572872 | tf_op jit(solution)/shard_map/ppermute | solution.py:29
  22.5 16.5 %collective-permute-start = (bf16[512,896]{1,0:T(8,128)(2,1)S(1)}, bf16[512,896]{1,0:T(8,128)(2,1)S(1)}, u32[]{:S(2)}, u32[]{:S(2)}) collective-permute-start(bf16[512,896]{1,0:T(8,128)(2,1)S(1)} %copy-done.1), channel_id=1, source_target_pairs={{0,1},{1,0},{2,3},{3,2},{4,5},{5,4},{6,7},{7,6},{8,9},{9,8},{10,11... | collective-permute-start | bytes 2752520 | tf_op jit(solution)/shard_map/ppermute | solution.py:18
  22.5 16.5 %collective-permute-start.13 = (bf16[2,512,256]{2,1,0:T(8,128)(2,1)S(1)}, bf16[2,512,256]{2,1,0:T(8,128)(2,1)}, u32[]{:S(2)}, u32[]{:S(2)}) collective-permute-start(bf16[2,512,256]{2,1,0:T(8,128)(2,1)S(1)} %collective-permute-done.12.refs_1_), channel_id=1, source_target_pairs={{0,2},{2,4},{4,6},{6,0},{1,7},{3,1},{5,3},{7,5},{8,10},{10,12},{12... | collective-permute-start | bytes 1572872 | tf_op jit(solution)/shard_map/ppermute | solution.py:29
  24.0 0.8 copy-start.2
  28.6 11.3 %collective-permute-start.15 = (bf16[2,512,256]{2,1,0:T(8,128)(2,1)}, bf16[2,512,256]{2,1,0:T(8,128)(2,1)}, u32[]{:S(2)}, u32[]{:S(2)}) collective-permute-start(bf16[2,512,256]{2,1,0:T(8,128)(2,1)} %collective-permute-done.11.refs_2_), channel_id=1, source_target_pairs={{0,2},{2,4},{4,6},{6,0},{1,7},{3,1},{5,3},{7,5},{8,10},{10,12},{12... | collective-permute-start | bytes 1572872 | tf_op jit(solution)/shard_map/ppermute | solution.py:29
  38.1 5.5 %collective-permute-start.24 = (bf16[512,896]{1,0:T(8,128)(2,1)}, bf16[512,896]{1,0:T(8,128)(2,1)}, u32[]{:S(2)}, u32[]{:S(2)}) collective-permute-start(bf16[512,896]{1,0:T(8,128)(2,1)} %collective-permute-done.23.refs_9_), channel_id=1, source_target_pairs={{0,1},{1,0},{2,3},{3,2},{4,5},{5,4},{6,7},{7,6},{8,9},{9,8},{10,11... | collective-permute-start | bytes 2752520 | tf_op jit(solution)/shard_map/ppermute | solution.py:18
  39.0 3.2 %collective-permute-start.16 = (bf16[2,512,256]{2,1,0:T(8,128)(2,1)}, bf16[2,512,256]{2,1,0:T(8,128)(2,1)}, u32[]{:S(2)}, u32[]{:S(2)}) collective-permute-start(bf16[2,512,256]{2,1,0:T(8,128)(2,1)} %collective-permute-done.11.refs_2_), channel_id=1, source_target_pairs={{0,1},{1,0},{2,3},{3,2},{4,5},{5,4},{6,7},{7,6},{8,9},{9,8},{10,11... | collective-permute-start | bytes 1572872 | tf_op jit(solution)/shard_map/ppermute | solution.py:18
  39.0 3.8 %collective-permute-start.14 = (bf16[2,512,256]{2,1,0:T(8,128)(2,1)}, bf16[2,512,256]{2,1,0:T(8,128)(2,1)S(1)}, u32[]{:S(2)}, u32[]{:S(2)}) collective-permute-start(bf16[2,512,256]{2,1,0:T(8,128)(2,1)} %collective-permute-done.13.refs_3_), channel_id=1, source_target_pairs={{0,1},{1,0},{2,3},{3,2},{4,5},{5,4},{6,7},{7,6},{8,9},{9,8},{10,11... | collective-permute-start | bytes 1572872 | tf_op jit(solution)/shard_map/ppermute | solution.py:18
  39.9 3.6 %collective-permute-start.17 = (bf16[2,512,256]{2,1,0:T(8,128)(2,1)}, bf16[2,512,256]{2,1,0:T(8,128)(2,1)S(1)}, u32[]{:S(2)}, u32[]{:S(2)}) collective-permute-start(bf16[2,512,256]{2,1,0:T(8,128)(2,1)} %collective-permute-done.15.refs_6_), channel_id=1, source_target_pairs={{0,1},{1,0},{2,3},{3,2},{4,5},{5,4},{6,7},{7,6},{8,9},{9,8},{10,11... | collective-permute-start | bytes 1572872 | tf_op jit(solution)/shard_map/ppermute | solution.py:18
  43.6 1.0 copy-start.3
  47.7 12.9 %collective-permute-start.25 = (f16[2,128,896]{2,1,0:T(8,128)(2,1)S(1)}, f16[2,128,896]{2,1,0:T(8,128)(2,1)S(1)}, u32[]{:S(2)}, u32[]{:S(2)}) collective-permute-start(f16[2,128,896]{2,1,0:T(8,128)(2,1)S(1)} %fusion.7), channel_id=1, source_target_pairs={{0,16},{16,32},{32,48},{48,64},{64,80},{80,96},{96,112},{112,0},{1... | collective-permute-start | bytes 1376264 | tf_op jit(solution)/shard_map/ppermute | solution.py:29
  60.5 2.8 %copy-start = (f32[3,2,256,896]{3,2,1,0:T(8,128)}, f32[3,2,256,896]{3,2,1,0:T(8,128)S(1)}, u32[]{:S(2)}) copy-start(f32[3,2,256,896]{3,2,1,0:T(8,128)S(1)} %get-tuple-element.14) | copy-start | bytes 16515076
  60.5 3.0 %copy-start.5 = (f32[256,896]{1,0:T(8,128)}, f32[256,896]{1,0:T(8,128)S(1)}, u32[]{:S(2)}) copy-start(f32[256,896]{1,0:T(8,128)S(1)} %get-tuple-element.13) | copy-start | bytes 2752516
  60.7 3.6 %copy-start.24 = (s32[8]{0:T(128)S(1)}, s32[8]{0:T(128)}, u32[]{:S(2)}) copy-start(s32[8]{0:T(128)} %constant.150.clone) | copy-start | bytes 100
  60.7 3.6 %copy-start.25 = (s32[8]{0:T(128)S(1)}, s32[8]{0:T(128)}, u32[]{:S(2)}) copy-start(s32[8]{0:T(128)} %constant.149.clone) | copy-start | bytes 100
  60.7 3.6 %copy-start.26 = (s32[8]{0:T(128)S(1)}, s32[8]{0:T(128)}, u32[]{:S(2)}) copy-start(s32[8]{0:T(128)} %constant.148.clone) | copy-start | bytes 100
  60.7 3.5 %copy-start.27 = (s32[8]{0:T(128)S(1)}, s32[8]{0:T(128)}, u32[]{:S(2)}) copy-start(s32[8]{0:T(128)} %constant.147.clone) | copy-start | bytes 100
  60.7 3.5 %copy-start.28 = (s32[8]{0:T(128)S(1)}, s32[8]{0:T(128)}, u32[]{:S(2)}) copy-start(s32[8]{0:T(128)} %constant.146.clone) | copy-start | bytes 100
  60.7 3.5 %copy-start.29 = (s32[8]{0:T(128)S(1)}, s32[8]{0:T(128)}, u32[]{:S(2)}) copy-start(s32[8]{0:T(128)} %constant.145.clone) | copy-start | bytes 100
  60.8 3.5 %copy-start.30 = (s32[8]{0:T(128)S(1)}, s32[8]{0:T(128)}, u32[]{:S(2)}) copy-start(s32[8]{0:T(128)} %constant.144.clone) | copy-start | bytes 100
  63.5 12.9 %collective-permute-start.26 = (f16[2,256,896]{2,1,0:T(8,128)(2,1)}, f16[2,256,896]{2,1,0:T(8,128)(2,1)}, u32[]{:S(2)}, u32[]{:S(2)}) collective-permute-start(f16[2,256,896]{2,1,0:T(8,128)(2,1)} %fusion), channel_id=1, source_target_pairs={{0,16},{16,32},{32,48},{48,64},{64,80},{80,96},{96,112},{112,0},{1... | collective-permute-start | bytes 2752520 | tf_op jit(solution)/shard_map/ppermute | solution.py:29
  64.3 11.0 %copy-start.9 = (bf16[512,256]{1,0:T(8,128)(2,1)S(1)}, bf16[512,256]{1,0:T(8,128)(2,1)}, u32[]{:S(2)}) copy-start(bf16[512,256]{1,0:T(8,128)(2,1)} %get-tuple-element.25) | copy-start | bytes 786436
  72.7 20.1 %collective-permute-start.2 = (f32[2,256,512]{2,1,0:T(8,128)}, f32[2,256,512]{2,1,0:T(8,128)}, u32[]{:S(2)}, u32[]{:S(2)}) collective-permute-start(f32[2,256,512]{2,1,0:T(8,128)} %get-tuple-element.11), channel_id=1, source_target_pairs={{0,2},{2,4},{4,6},{6,0},{1,7},{3,1},{5,3},{7,5},{8,10},{10,12},{12... | collective-permute-start | bytes 3145736 | tf_op jit(solution)/shard_map/ppermute | solution.py:29
  75.3 17.6 %copy-start.11 = (f32[2,256,512]{2,1,0:T(8,128)S(1)}, f32[2,256,512]{2,1,0:T(8,128)}, u32[]{:S(2)}) copy-start(f32[2,256,512]{2,1,0:T(8,128)} %get-tuple-element.12) | copy-start | bytes 3145732
  75.3 6.0 %collective-permute-start.18 = (bf16[512,256]{1,0:T(8,128)(2,1)S(1)}, bf16[512,256]{1,0:T(8,128)(2,1)S(1)}, u32[]{:S(2)}, u32[]{:S(2)}) collective-permute-start(bf16[512,256]{1,0:T(8,128)(2,1)S(1)} %copy-done.9), channel_id=1, source_target_pairs={{0,1},{1,0},{2,3},{3,2},{4,5},{5,4},{6,7},{7,6},{8,9},{9,8},{10,11... | collective-permute-start | bytes 786440 | tf_op jit(solution)/shard_map/ppermute | solution.py:18
  79.4 20.6 %collective-permute-start.27 = (f16[2,256,896]{2,1,0:T(8,128)(2,1)}, f16[2,256,896]{2,1,0:T(8,128)(2,1)}, u32[]{:S(2)}, u32[]{:S(2)}) collective-permute-start(f16[2,256,896]{2,1,0:T(8,128)(2,1)} %fusion.1), channel_id=1, source_target_pairs={{0,16},{16,32},{32,48},{48,64},{64,80},{80,96},{96,112},{112,0},{1... | collective-permute-start | bytes 2752520 | tf_op jit(solution)/shard_map/ppermute | solution.py:29
  81.3 14.8 %copy-start.13 = (bf16[512,256]{1,0:T(8,128)(2,1)}, bf16[512,256]{1,0:T(8,128)(2,1)S(1)}, u32[]{:S(2)}) copy-start(bf16[512,256]{1,0:T(8,128)(2,1)S(1)} %collective-permute-done.18) | copy-start | bytes 786436
  81.4 11.5 %collective-permute-start.19 = (bf16[2,512,256]{2,1,0:T(8,128)(2,1)S(1)}, bf16[2,512,256]{2,1,0:T(8,128)(2,1)}, u32[]{:S(2)}, u32[]{:S(2)}) collective-permute-start(bf16[2,512,256]{2,1,0:T(8,128)(2,1)S(1)} %pad_maximum_fusion.5), channel_id=1, source_target_pairs={{0,2},{2,4},{4,6},{6,0},{1,7},{3,1},{5,3},{7,5},{8,10},{10,12},{12... | collective-permute-start | bytes 1572872 | tf_op jit(solution)/shard_map/ppermute | solution.py:29
  92.9 23.8 %collective-permute-start.20 = (bf16[2,512,256]{2,1,0:T(8,128)(2,1)}, bf16[2,512,256]{2,1,0:T(8,128)(2,1)}, u32[]{:S(2)}, u32[]{:S(2)}) collective-permute-start(bf16[2,512,256]{2,1,0:T(8,128)(2,1)} %collective-permute-done.19), channel_id=1, source_target_pairs={{0,1},{1,0},{2,3},{3,2},{4,5},{5,4},{6,7},{7,6},{8,9},{9,8},{10,11... | collective-permute-start | bytes 1572872 | tf_op jit(solution)/shard_map/ppermute | solution.py:18
  96.1 9.8 %copy-start.18 = (s32[16]{0:T(128)S(1)}, s32[16]{0:T(128)}, u32[]{:S(2)}) copy-start(s32[16]{0:T(128)} %constant.159.clone) | copy-start | bytes 196
  96.1 9.8 %copy-start.19 = (s32[16]{0:T(128)S(1)}, s32[16]{0:T(128)}, u32[]{:S(2)}) copy-start(s32[16]{0:T(128)} %constant.158.clone) | copy-start | bytes 196
  96.1 9.8 %copy-start.20 = (s32[16]{0:T(128)S(1)}, s32[16]{0:T(128)}, u32[]{:S(2)}) copy-start(s32[16]{0:T(128)} %constant.157.clone) | copy-start | bytes 196
  96.1 9.8 %copy-start.21 = (s32[16]{0:T(128)S(1)}, s32[16]{0:T(128)}, u32[]{:S(2)}) copy-start(s32[16]{0:T(128)} %constant.156.clone) | copy-start | bytes 196
  96.2 9.8 %copy-start.22 = (s32[16]{0:T(128)S(1)}, s32[16]{0:T(128)}, u32[]{:S(2)}) copy-start(s32[16]{0:T(128)} %constant.155.clone) | copy-start | bytes 196
  96.2 9.8 %copy-start.23 = (s32[16]{0:T(128)S(1)}, s32[16]{0:T(128)}, u32[]{:S(2)}) copy-start(s32[16]{0:T(128)} %constant.154.clone) | copy-start | bytes 196
  96.2 10.3 %copy-start.4 = (bf16[2,512,256]{2,1,0:T(8,128)(2,1)S(1)}, bf16[2,512,256]{2,1,0:T(8,128)(2,1)}, u32[]{:S(2)}) copy-start(bf16[2,512,256]{2,1,0:T(8,128)(2,1)} %copy-done.2) | copy-start | bytes 1572868
  96.2 23.7 %collective-permute-start.5 = (f32[2,256,512]{2,1,0:T(8,128)}, f32[2,256,512]{2,1,0:T(8,128)S(1)}, u32[]{:S(2)}, u32[]{:S(2)}) collective-permute-start(f32[2,256,512]{2,1,0:T(8,128)} %get-tuple-element.19), channel_id=1, source_target_pairs={{0,2},{2,4},{4,6},{6,0},{1,7},{3,1},{5,3},{7,5},{8,10},{10,12},{12... | collective-permute-start | bytes 3145736 | tf_op jit(solution)/shard_map/ppermute | solution.py:29
  103.0 18.2 %collective-permute-start.28 = (f16[2,256,896]{2,1,0:T(8,128)(2,1)}, f16[2,256,896]{2,1,0:T(8,128)(2,1)}, u32[]{:S(2)}, u32[]{:S(2)}) collective-permute-start(f16[2,256,896]{2,1,0:T(8,128)(2,1)} %fusion.2), channel_id=1, source_target_pairs={{0,16},{16,32},{32,48},{48,64},{64,80},{80,96},{96,112},{112,0},{1... | collective-permute-start | bytes 2752520 | tf_op jit(solution)/shard_map/ppermute | solution.py:29
  105.3 9.6 %collective-permute-start.21 = (bf16[512,256]{1,0:T(8,128)(2,1)}, bf16[512,256]{1,0:T(8,128)(2,1)}, u32[]{:S(2)}, u32[]{:S(2)}) collective-permute-start(bf16[512,256]{1,0:T(8,128)(2,1)} %get-tuple-element.21), channel_id=1, source_target_pairs={{0,2},{2,4},{4,6},{6,0},{1,7},{3,1},{5,3},{7,5},{8,10},{10,12},{12... | collective-permute-start | bytes 786440 | tf_op jit(solution)/shard_map/ppermute | solution.py:29
  105.7 20.4 %collective-permute-start.3 = (f32[2,256,512]{2,1,0:T(8,128)}, f32[2,256,512]{2,1,0:T(8,128)S(1)}, u32[]{:S(2)}, u32[]{:S(2)}) collective-permute-start(f32[2,256,512]{2,1,0:T(8,128)} %get-tuple-element.18), channel_id=1, source_target_pairs={{0,2},{2,4},{4,6},{6,0},{1,7},{3,1},{5,3},{7,5},{8,10},{10,12},{12... | collective-permute-start | bytes 3145736 | tf_op jit(solution)/shard_map/ppermute | solution.py:29
  106.5 11.3 %copy-start.12 = (bf16[1,512,256]{2,1,0:T(8,128)(2,1)S(1)}, bf16[1,512,256]{2,1,0:T(8,128)(2,1)}, u32[]{:S(2)}) copy-start(bf16[1,512,256]{2,1,0:T(8,128)(2,1)} %get-tuple-element.22) | copy-start | bytes 786436
  114.9 5.2 %collective-permute-start.22 = (bf16[512,256]{1,0:T(8,128)(2,1)}, bf16[512,256]{1,0:T(8,128)(2,1)S(1)}, u32[]{:S(2)}, u32[]{:S(2)}) collective-permute-start(bf16[512,256]{1,0:T(8,128)(2,1)} %collective-permute-done.21), channel_id=1, source_target_pairs={{0,1},{1,0},{2,3},{3,2},{4,5},{5,4},{6,7},{7,6},{8,9},{9,8},{10,11... | collective-permute-start | bytes 786440 | tf_op jit(solution)/shard_map/ppermute | solution.py:18
  117.8 2.3 %copy-start.14 = (bf16[512,256]{1,0:T(8,128)(2,1)S(1)}, bf16[512,256]{1,0:T(8,128)(2,1)}, u32[]{:S(2)}) copy-start(bf16[512,256]{1,0:T(8,128)(2,1)} %copy-done.13) | copy-start | bytes 786436
  119.9 1.9 %copy-start.8 = (bf16[1,512,256]{2,1,0:T(8,128)(2,1)S(1)}, bf16[1,512,256]{2,1,0:T(8,128)(2,1)}, u32[]{:S(2)}) copy-start(bf16[1,512,256]{2,1,0:T(8,128)(2,1)} %copy-done.7) | copy-start | bytes 786436
  119.9 8.0 %collective-permute-start.6 = (f32[256,512]{1,0:T(8,128)S(1)}, f32[256,512]{1,0:T(8,128)S(1)}, u32[]{:S(2)}, u32[]{:S(2)}) collective-permute-start(f32[256,512]{1,0:T(8,128)S(1)} %dynamic-slice_bitcast_fusion), channel_id=1, source_target_pairs={{0,1},{1,0},{2,3},{3,2},{4,5},{5,4},{6,7},{7,6},{8,9},{9,8},{10,11... | collective-permute-start | bytes 1572872 | tf_op jit(solution)/shard_map/ppermute | solution.py:18
  121.2 34.4 %collective-permute-start.29 = (f16[2,256,896]{2,1,0:T(8,128)(2,1)}, f16[2,256,896]{2,1,0:T(8,128)(2,1)}, u32[]{:S(2)}, u32[]{:S(2)}) collective-permute-start(f16[2,256,896]{2,1,0:T(8,128)(2,1)} %collective-permute-done.28), channel_id=1, source_target_pairs={{0,1},{1,0},{2,3},{3,2},{4,5},{5,4},{6,7},{7,6},{8,9},{9,8},{10,11... | collective-permute-start | bytes 2752520 | tf_op jit(solution)/shard_map/ppermute | solution.py:18
  122.9 5.1 %copy-start.10 = (f32[2,256,512]{2,1,0:T(8,128)S(1)}, f32[2,256,512]{2,1,0:T(8,128)}, u32[]{:S(2)}) copy-start(f32[2,256,512]{2,1,0:T(8,128)} %get-tuple-element.9) | copy-start | bytes 3145732
  126.1 31.8 %collective-permute-start.4 = (f32[256,512]{1,0:T(8,128)S(1)}, f32[256,512]{1,0:T(8,128)S(1)}, u32[]{:S(2)}, u32[]{:S(2)}) collective-permute-start(f32[256,512]{1,0:T(8,128)S(1)} %dynamic-slice_bitcast_fusion.1), channel_id=1, source_target_pairs={{0,1},{1,0},{2,3},{3,2},{4,5},{5,4},{6,7},{7,6},{8,9},{9,8},{10,11... | collective-permute-start | bytes 1572872 | tf_op jit(solution)/shard_map/ppermute | solution.py:18
  128.1 27.6 %copy-start.6 = (f32[256,896]{1,0:T(8,128)S(1)}, f32[256,896]{1,0:T(8,128)}, u32[]{:S(2)}) copy-start(f32[256,896]{1,0:T(8,128)} %copy-done.5) | copy-start | bytes 2752516
  128.1 30.2 %collective-permute-start.7 = (f32[256,512]{1,0:T(8,128)S(1)}, f32[256,512]{1,0:T(8,128)S(1)}, u32[]{:S(2)}, u32[]{:S(2)}) collective-permute-start(f32[256,512]{1,0:T(8,128)S(1)} %fusion.3), channel_id=1, source_target_pairs={{0,8},{8,0},{1,9},{9,1},{2,10},{10,2},{3,11},{11,3},{4,12},{12,4},... | collective-permute-start | bytes 1572872 | tf_op jit(solution)/shard_map/ppermute | solution.py:18
